TPU v7x, 16 devices: a whole 2x2x2 slice. The times are simulated.
16 devices in a mesh: data: 4 (over z, y), stage: 4 (over x, core).
Axes of the slice: x: 2, y: 2, z: 2, core: 2. Of those that a mesh axis runs over, the one named last changes fastest.
Arguments:
- master_up: float32 [4, 256, 1024], P('stage')
- master_down: float32 [4, 1024, 256], P('stage')
- mom1_up: float32 [4, 256, 1024], P('stage')
- mom1_down: float32 [4, 1024, 256], P('stage')
- mom2_up: float32 [4, 256, 1024], P('stage')
- mom2_down: float32 [4, 1024, 256], P('stage')
- grad_up: float32 [4, 4, 256, 1024], P('data', 'stage')
- grad_down: float32 [4, 4, 1024, 256], P('data', 'stage')
- stage_acts: bfloat16 [4, 4096, 256], P('stage', 'data')
- loss_grad: bfloat16 [4096, 256], P('data')
- next_batch: bfloat16 [16, 4096, 256], P(None, 'data')
- learn_rate: float32 [], replicated
- max_norm: float32 [], replicated
Outputs:
- output 1: float32 [4, 256, 1024], P('stage')
- output 2: float32 [4, 1024, 256], P('stage')
- output 3: float32 [4, 256, 1024], P('stage')
- output 4: float32 [4, 1024, 256], P('stage')
- output 5: float32 [4, 256, 1024], P('stage')
- output 6: float32 [4, 1024, 256], P('stage')
- output 7: bfloat16 [4, 16, 4096, 256], P('stage', None, 'data')
All inputs are finite; a program needn't handle non-finite values.
Results may differ from a plain program's by a relative error of at most 0.00850932.
Values are sent between devices in bfloat16 or wider.
A program may use at most 1 GiB of HBM per device.

v0:
```python
import jax
import jax.numpy as jnp
from jax import lax
from jax.sharding import PartitionSpec as P

BETA1 = 0.9
BETA2 = 0.95
ADAM_EPS = 1e-8
WEIGHT_DECAY = 0.1
NORM_EPS = 1e-6
ADAM_STEP = 8
SQRT_TWO_PI = 0.7978845608028654
GELU_CUBIC = 0.044715


def tanh_part(pre_act):
    return jnp.tanh(SQRT_TWO_PI * (pre_act + GELU_CUBIC * pre_act * pre_act * pre_act))


def gelu_tanh(pre_act):
    return 0.5 * pre_act * (1.0 + tanh_part(pre_act))


def gelu_pair(pre_act):
    tanh_val = tanh_part(pre_act)
    act_value = 0.5 * pre_act * (1.0 + tanh_val)
    act_slope = 0.5 * (1.0 + tanh_val) + 0.5 * pre_act * (1.0 - tanh_val * tanh_val) * SQRT_TWO_PI * (1.0 + 3.0 * GELU_CUBIC * pre_act * pre_act)
    return act_value, act_slope


def mat_tn(left, right):
    return lax.dot_general(left, right, (((0,), (0,)), ((), ())), preferred_element_type=jnp.float32)


def mat_nt(left, right):
    return lax.dot_general(left, right, (((1,), (1,)), ((), ())), preferred_element_type=jnp.float32)


def adamw_update(master, first_mom, second_mom, grad_avg, clip_scale, learn_rate):
    scaled = clip_scale * grad_avg
    new_first = BETA1 * first_mom + (1.0 - BETA1) * scaled
    new_second = BETA2 * second_mom + (1.0 - BETA2) * scaled * scaled
    first_hat = new_first / (1.0 - BETA1 ** ADAM_STEP)
    second_hat = new_second / (1.0 - BETA2 ** ADAM_STEP)
    new_master = master - learn_rate * (first_hat / (jnp.sqrt(second_hat) + ADAM_EPS) + WEIGHT_DECAY * master)
    return new_master, new_first, new_second


def stage_forward(rows_in, up_bf, down_bf):
    pre_act = jnp.dot(rows_in, up_bf, preferred_element_type=jnp.float32)
    hidden = gelu_tanh(pre_act).astype(jnp.bfloat16)
    return (rows_in.astype(jnp.float32) + jnp.dot(hidden, down_bf, preferred_element_type=jnp.float32)).astype(jnp.bfloat16)


def solution(mesh):
    n_stages = mesh.shape['stage']
    n_reps = mesh.shape['data']
    last_stage = n_stages - 1
    down_pairs = [(source, source - 1) for source in range(1, n_stages)]
    up_pairs = [(source, source + 1) for source in range(n_stages - 1)]

    def local_step(master_up, master_down, mom1_up, mom1_down, mom2_up, mom2_down, grad_up, grad_down, stage_acts, loss_grad, next_batch, learn_rate, max_norm):
        stage_idx = lax.axis_index('stage')
        stage_in = stage_acts[0]
        up_bf = master_up[0].astype(jnp.bfloat16)
        down_bf = master_down[0].astype(jnp.bfloat16)
        tok_rows, model_width = stage_in.shape
        hidden_width = up_bf.shape[1]

        def local_back(grad_in):
            pre_act = jnp.dot(stage_in, up_bf, preferred_element_type=jnp.float32)
            act_value, act_slope = gelu_pair(pre_act)
            d_pre = (mat_nt(grad_in, down_bf) * act_slope).astype(jnp.bfloat16)
            return act_value.astype(jnp.bfloat16), d_pre

        def back_run(operands):
            grad_in = operands[0]
            hidden, d_pre = local_back(grad_in)
            d_rows = (grad_in.astype(jnp.float32) + mat_nt(d_pre, up_bf)).astype(jnp.bfloat16)
            return d_rows, grad_in, hidden, d_pre

        def back_skip(operands):
            return jnp.zeros_like(operands[0]), operands[1], operands[2], operands[3]

        def back_tick(step_idx, carry):
            received, grad_own, hid_own, dpre_own = carry
            grad_in = jnp.where(step_idx == 0, loss_grad, received)
            d_rows, grad_own, hid_own, dpre_own = lax.cond(stage_idx == last_stage - step_idx, back_run, back_skip, (grad_in, grad_own, hid_own, dpre_own))
            return lax.ppermute(d_rows, 'stage', down_pairs), grad_own, hid_own, dpre_own

        row_zeros = jnp.zeros((tok_rows, model_width), jnp.bfloat16)
        wide_zeros = jnp.zeros((tok_rows, hidden_width), jnp.bfloat16)
        received, grad_own, hid_own, dpre_own = lax.fori_loop(0, last_stage, back_tick, (row_zeros, row_zeros, wide_zeros, wide_zeros))

        def first_run(operands):
            hidden, d_pre = local_back(operands[0])
            return operands[0], hidden, d_pre

        def first_skip(operands):
            return operands[1], operands[2], operands[3]

        grad_own, hid_own, dpre_own = lax.cond(stage_idx == 0, first_run, first_skip, (received, grad_own, hid_own, dpre_own))

        gbar_up = lax.psum(grad_up[0, 0] + mat_tn(stage_in, dpre_own), 'data') / n_reps
        gbar_down = lax.psum(grad_down[0, 0] + mat_tn(hid_own, grad_own), 'data') / n_reps
        local_sq = jnp.sum(gbar_up * gbar_up) + jnp.sum(gbar_down * gbar_down)
        grad_norm = jnp.sqrt(lax.psum(local_sq, 'stage'))
        clip_scale = jnp.minimum(1.0, max_norm / (grad_norm + NORM_EPS))
        new_up, new_m1_up, new_m2_up = adamw_update(master_up[0], mom1_up[0], mom2_up[0], gbar_up, clip_scale, learn_rate)
        new_down, new_m1_down, new_m2_down = adamw_update(master_down[0], mom1_down[0], mom2_down[0], gbar_down, clip_scale, learn_rate)
        new_up_bf = new_up.astype(jnp.bfloat16)
        new_down_bf = new_down.astype(jnp.bfloat16)
        n_micro = next_batch.shape[0]
        n_ticks = n_micro + last_stage

        def fwd_compute(tick_idx, received, stage_outs):
            micro_idx = tick_idx - stage_idx
            safe_idx = jnp.clip(micro_idx, 0, n_micro - 1)
            first_in = lax.dynamic_index_in_dim(next_batch, safe_idx, 0, keepdims=False)
            rows_in = jnp.where(stage_idx == 0, first_in, received)

            def fwd_run(operands):
                rows_out = stage_forward(operands[0], new_up_bf, new_down_bf)
                return rows_out, lax.dynamic_update_index_in_dim(operands[1], rows_out, safe_idx, 0)

            def fwd_skip(operands):
                return jnp.zeros_like(operands[0]), operands[1]

            active = (micro_idx >= 0) & (micro_idx < n_micro)
            return lax.cond(active, fwd_run, fwd_skip, (rows_in, stage_outs))

        def fwd_tick(tick_idx, carry):
            rows_out, stage_outs = fwd_compute(tick_idx, carry[0], carry[1])
            return lax.ppermute(rows_out, 'stage', up_pairs), stage_outs

        outs_init = jnp.zeros((n_micro, tok_rows, model_width), jnp.bfloat16)
        received, stage_outs = lax.fori_loop(0, n_ticks - 1, fwd_tick, (row_zeros, outs_init))
        _, stage_outs = fwd_compute(n_ticks - 1, received, stage_outs)
        return (new_up[None], new_down[None], new_m1_up[None], new_m1_down[None], new_m2_up[None], new_m2_down[None], stage_outs[None])

    w_spec = P('stage', None, None)
    g_spec = P('data', 'stage', None, None)
    in_specs = (w_spec, w_spec, w_spec, w_spec, w_spec, w_spec, g_spec, g_spec, P('stage', 'data', None), P('data', None), P(None, 'data', None), P(), P())
    out_specs = (w_spec, w_spec, w_spec, w_spec, w_spec, w_spec, P('stage', None, 'data', None))
    return jax.shard_map(local_step, mesh=mesh, in_specs=in_specs, out_specs=out_specs, check_vma=False)
```

profile of v0, /device:TPU:3, one launch (start us, length us, event | category | flops | bytes accessed | tf_op | source)
XLA Modules:
  0.0 440.1 jit_solution(17412462468239492916)
XLA Ops:
  14.9 38.3 %while.41 = (s32[]{:T(128)}, bf16[1024,256]{1,0:T(8,128)(2,1)S(1)}, bf16[1024,256]{1,0:T(8,128)(2,1)}, bf16[1024,1024]{1,0:T(8,128)(2,1)}, bf16[1024,1024]{1,0:T...) while((s32[]{:T(128)}, bf16[1024,256]{1,0:T(8,128)(2,1)S(1)}, ...), condition=%wide.region_3.4_spmd, body=%wide.region_0.3_spmd.sunk | while | flops 1641021440 | bytes 36700568 | solution.py:93
  14.9 11.6 %conditional.8 = (bf16[1024,256]{1,0:T(8,128)(2,1)S(1)}, bf16[1024,256]{1,0:T(8,128)(2,1)}, bf16[1024,1024]{1,0:T(8,128)(2,1)}, bf16[1024,1024]{1,0:T(8,128)(2,1)}) conditional(s32[]{:T(128)} %convert_element_type.137, (bf16[1024,256]{1,0:T(8,128)(2,1)}, bf16[1024,1024]{1,0:T(8,128)(2,1)}, bf16[1024,1024]{1,0:T(8,128)(2,1)}) %tuple.133, (s32[]{:T(128)}, ...), branch_computations={%region_1.1_spmd, %region_2.2_spmd} | conditional | flops 1641021440 | bytes 34603160 | solution.py:88
  29.3 13.8 %collective-permute-start = (bf16[1024,256]{1,0:T(8,128)(2,1)S(1)}, bf16[1024,256]{1,0:T(8,128)(2,1)S(1)}, u32[]{:S(2)}, u32[]{:S(2)}) collective-permute-start(bf16[1024,256]{1,0:T(8,128)(2,1)S(1)} %get-tuple-element.784), channel_id=1, source_target_pairs={{1,0},{2,1},{3,2},{5,4},{6,5},{7,6},{9,8},{10,9},{11,10},{13,12},{... | collective-permute-start | bytes 1572872 | tf_op jit(solution)/shard_map/while/body/eval_jaxpr/ppermute | solution.py:89
  44.6 7.1 %collective-permute-start = (bf16[1024,256]{1,0:T(8,128)(2,1)S(1)}, bf16[1024,256]{1,0:T(8,128)(2,1)S(1)}, u32[]{:S(2)}, u32[]{:S(2)}) collective-permute-start(bf16[1024,256]{1,0:T(8,128)(2,1)S(1)} %get-tuple-element.784), channel_id=1, source_target_pairs={{1,0},{2,1},{3,2},{5,4},{6,5},{7,6},{9,8},{10,9},{11,10},{13,12},{... | collective-permute-start | bytes 1572872 | tf_op jit(solution)/shard_map/while/body/eval_jaxpr/ppermute | solution.py:89
  66.6 77.4 %all-reduce.3.cloned.1.call-done = (f32[256,1024]{0,1:T(8,128)}, f32[1024,256]{1,0:T(8,128)}) async-done(((f32[256,1024]{0,1:T(8,128)}, f32[1024,256]{1,0:T(8,128)}), (f32[256,1024]{0,1:T(8,128)}, f32[1024,256]{1,0:T(8,128)})) %all-reduce.3.cloned.1.call-update) | async-done | bytes 2097168 | tf_op jit(solution)/shard_map/psum | solution.py:104
  149.5 6.6 %psum.23 = f32[]{:T(128)} all-reduce(f32[]{:T(128)S(6)} %add.172), channel_id=1, replica_groups=mesh['data'=4,'stage'=4] {'stage'}, use_global_device_ids=true, to_apply=%region_10.11 | all-reduce | flops 1 | bytes 8 | tf_op jit(solution)/shard_map/psum | solution.py:107
  172.8 251.2 %while.42 = (s32[]{:T(128)}, bf16[1024,256]{1,0:T(8,128)(2,1)}, bf16[16,1024,256]{2,1,0:T(8,128)(2,1)}, s32[]{:T(128)}, pred[]{:T(512)}, /*index=5*/bf16[16,1024...) while((s32[]{:T(128)}, bf16[1024,256]{1,0:T(8,128)(2,1)}, ...), condition=%wide.region_14.15_spmd, body=%wide.region_11.14_spmd.sunk | while | flops 1084489728 | bytes 6293787 | solution.py:137
  178.5 9.2 %collective-permute-done.1 = bf16[1024,256]{1,0:T(8,128)(2,1)} collective-permute-done((bf16[1024,256]{1,0:T(8,128)(2,1)S(1)}, bf16[1024,256]{1,0:T(8,128)(2,1)}, u32[]{:S(2)}, u32[]{:S(2)}) %collective-permute-start.1) | collective-permute-done | bytes 524320 | tf_op jit(solution)/shard_map/while/body/eval_jaxpr/ppermute | solution.py:134
  189.1 15.1 %collective-permute-done.1 = bf16[1024,256]{1,0:T(8,128)(2,1)} collective-permute-done((bf16[1024,256]{1,0:T(8,128)(2,1)S(1)}, bf16[1024,256]{1,0:T(8,128)(2,1)}, u32[]{:S(2)}, u32[]{:S(2)}) %collective-permute-start.1) | collective-permute-done | bytes 524320 | tf_op jit(solution)/shard_map/while/body/eval_jaxpr/ppermute | solution.py:134
  209.8 9.1 %collective-permute-done.1 = bf16[1024,256]{1,0:T(8,128)(2,1)} collective-permute-done((bf16[1024,256]{1,0:T(8,128)(2,1)S(1)}, bf16[1024,256]{1,0:T(8,128)(2,1)}, u32[]{:S(2)}, u32[]{:S(2)}) %collective-permute-start.1) | collective-permute-done | bytes 524320 | tf_op jit(solution)/shard_map/while/body/eval_jaxpr/ppermute | solution.py:134
  224.3 9.2 %collective-permute-done.1 = bf16[1024,256]{1,0:T(8,128)(2,1)} collective-permute-done((bf16[1024,256]{1,0:T(8,128)(2,1)S(1)}, bf16[1024,256]{1,0:T(8,128)(2,1)}, u32[]{:S(2)}, u32[]{:S(2)}) %collective-permute-start.1) | collective-permute-done | bytes 524320 | tf_op jit(solution)/shard_map/while/body/eval_jaxpr/ppermute | solution.py:134
  239.0 9.2 %collective-permute-done.1 = bf16[1024,256]{1,0:T(8,128)(2,1)} collective-permute-done((bf16[1024,256]{1,0:T(8,128)(2,1)S(1)}, bf16[1024,256]{1,0:T(8,128)(2,1)}, u32[]{:S(2)}, u32[]{:S(2)}) %collective-permute-start.1) | collective-permute-done | bytes 524320 | tf_op jit(solution)/shard_map/while/body/eval_jaxpr/ppermute | solution.py:134
  253.6 9.2 %collective-permute-done.1 = bf16[1024,256]{1,0:T(8,128)(2,1)} collective-permute-done((bf16[1024,256]{1,0:T(8,128)(2,1)S(1)}, bf16[1024,256]{1,0:T(8,128)(2,1)}, u32[]{:S(2)}, u32[]{:S(2)}) %collective-permute-start.1) | collective-permute-done | bytes 524320 | tf_op jit(solution)/shard_map/while/body/eval_jaxpr/ppermute | solution.py:134
  268.3 9.2 %collective-permute-done.1 = bf16[1024,256]{1,0:T(8,128)(2,1)} collective-permute-done((bf16[1024,256]{1,0:T(8,128)(2,1)S(1)}, bf16[1024,256]{1,0:T(8,128)(2,1)}, u32[]{:S(2)}, u32[]{:S(2)}) %collective-permute-start.1) | collective-permute-done | bytes 524320 | tf_op jit(solution)/shard_map/while/body/eval_jaxpr/ppermute | solution.py:134
  282.9 9.2 %collective-permute-done.1 = bf16[1024,256]{1,0:T(8,128)(2,1)} collective-permute-done((bf16[1024,256]{1,0:T(8,128)(2,1)S(1)}, bf16[1024,256]{1,0:T(8,128)(2,1)}, u32[]{:S(2)}, u32[]{:S(2)}) %collective-permute-start.1) | collective-permute-done | bytes 524320 | tf_op jit(solution)/shard_map/while/body/eval_jaxpr/ppermute | solution.py:134
  297.6 9.2 %collective-permute-done.1 = bf16[1024,256]{1,0:T(8,128)(2,1)} collective-permute-done((bf16[1024,256]{1,0:T(8,128)(2,1)S(1)}, bf16[1024,256]{1,0:T(8,128)(2,1)}, u32[]{:S(2)}, u32[]{:S(2)}) %collective-permute-start.1) | collective-permute-done | bytes 524320 | tf_op jit(solution)/shard_map/while/body/eval_jaxpr/ppermute | solution.py:134
  312.2 9.2 %collective-permute-done.1 = bf16[1024,256]{1,0:T(8,128)(2,1)} collective-permute-done((bf16[1024,256]{1,0:T(8,128)(2,1)S(1)}, bf16[1024,256]{1,0:T(8,128)(2,1)}, u32[]{:S(2)}, u32[]{:S(2)}) %collective-permute-start.1) | collective-permute-done | bytes 524320 | tf_op jit(solution)/shard_map/while/body/eval_jaxpr/ppermute | solution.py:134
  326.9 9.2 %collective-permute-done.1 = bf16[1024,256]{1,0:T(8,128)(2,1)} collective-permute-done((bf16[1024,256]{1,0:T(8,128)(2,1)S(1)}, bf16[1024,256]{1,0:T(8,128)(2,1)}, u32[]{:S(2)}, u32[]{:S(2)}) %collective-permute-start.1) | collective-permute-done | bytes 524320 | tf_op jit(solution)/shard_map/while/body/eval_jaxpr/ppermute | solution.py:134
  341.5 9.2 %collective-permute-done.1 = bf16[1024,256]{1,0:T(8,128)(2,1)} collective-permute-done((bf16[1024,256]{1,0:T(8,128)(2,1)S(1)}, bf16[1024,256]{1,0:T(8,128)(2,1)}, u32[]{:S(2)}, u32[]{:S(2)}) %collective-permute-start.1) | collective-permute-done | bytes 524320 | tf_op jit(solution)/shard_map/while/body/eval_jaxpr/ppermute | solution.py:134
  356.2 9.2 %collective-permute-done.1 = bf16[1024,256]{1,0:T(8,128)(2,1)} collective-permute-done((bf16[1024,256]{1,0:T(8,128)(2,1)S(1)}, bf16[1024,256]{1,0:T(8,128)(2,1)}, u32[]{:S(2)}, u32[]{:S(2)}) %collective-permute-start.1) | collective-permute-done | bytes 524320 | tf_op jit(solution)/shard_map/while/body/eval_jaxpr/ppermute | solution.py:134
  370.8 9.2 %collective-permute-done.1 = bf16[1024,256]{1,0:T(8,128)(2,1)} collective-permute-done((bf16[1024,256]{1,0:T(8,128)(2,1)S(1)}, bf16[1024,256]{1,0:T(8,128)(2,1)}, u32[]{:S(2)}, u32[]{:S(2)}) %collective-permute-start.1) | collective-permute-done | bytes 524320 | tf_op jit(solution)/shard_map/while/body/eval_jaxpr/ppermute | solution.py:134
  385.5 9.2 %collective-permute-done.1 = bf16[1024,256]{1,0:T(8,128)(2,1)} collective-permute-done((bf16[1024,256]{1,0:T(8,128)(2,1)S(1)}, bf16[1024,256]{1,0:T(8,128)(2,1)}, u32[]{:S(2)}, u32[]{:S(2)}) %collective-permute-start.1) | collective-permute-done | bytes 524320 | tf_op jit(solution)/shard_map/while/body/eval_jaxpr/ppermute | solution.py:134
  400.2 9.2 %collective-permute-done.1 = bf16[1024,256]{1,0:T(8,128)(2,1)} collective-permute-done((bf16[1024,256]{1,0:T(8,128)(2,1)S(1)}, bf16[1024,256]{1,0:T(8,128)(2,1)}, u32[]{:S(2)}, u32[]{:S(2)}) %collective-permute-start.1) | collective-permute-done | bytes 524320 | tf_op jit(solution)/shard_map/while/body/eval_jaxpr/ppermute | solution.py:134
  414.8 9.2 %collective-permute-done.1 = bf16[1024,256]{1,0:T(8,128)(2,1)} collective-permute-done((bf16[1024,256]{1,0:T(8,128)(2,1)S(1)}, bf16[1024,256]{1,0:T(8,128)(2,1)}, u32[]{:S(2)}, u32[]{:S(2)}) %collective-permute-start.1) | collective-permute-done | bytes 524320 | tf_op jit(solution)/shard_map/while/body/eval_jaxpr/ppermute | solution.py:134
  (127 shorter events, 221.9 us)
Async XLA Ops:
  7.2 136.8 %all-reduce.3.cloned.1.call-start = ((), (), s32[]{:S(2)}) async-start(), calls=%async_computation | async-start | bytes 4194304 | tf_op jit(solution)/shard_map/psum | solution.py:104
  14.9 40.9 %copy-start.5 = (bf16[256,1024]{0,1:T(8,128)(2,1)S(1)}, bf16[256,1024]{0,1:T(8,128)(2,1)}, u32[]{:S(2)}) copy-start(bf16[256,1024]{0,1:T(8,128)(2,1)} %copy-done.4) | copy-start | bytes 1572868
  26.4 2.8 collective-permute-start
  29.3 15.3 %collective-permute-start = (bf16[1024,256]{1,0:T(8,128)(2,1)S(1)}, bf16[1024,256]{1,0:T(8,128)(2,1)S(1)}, u32[]{:S(2)}, u32[]{:S(2)}) collective-permute-start(bf16[1024,256]{1,0:T(8,128)(2,1)S(1)} %get-tuple-element.784), channel_id=1, source_target_pairs={{1,0},{2,1},{3,2},{5,4},{6,5},{7,6},{9,8},{10,9},{11,10},{13,12},{... | collective-permute-start | bytes 1572872 | tf_op jit(solution)/shard_map/while/body/eval_jaxpr/ppermute | solution.py:89
  44.6 8.6 %collective-permute-start = (bf16[1024,256]{1,0:T(8,128)(2,1)S(1)}, bf16[1024,256]{1,0:T(8,128)(2,1)S(1)}, u32[]{:S(2)}, u32[]{:S(2)}) collective-permute-start(bf16[1024,256]{1,0:T(8,128)(2,1)S(1)} %get-tuple-element.784), channel_id=1, source_target_pairs={{1,0},{2,1},{3,2},{5,4},{6,5},{7,6},{9,8},{10,9},{11,10},{13,12},{... | collective-permute-start | bytes 1572872 | tf_op jit(solution)/shard_map/while/body/eval_jaxpr/ppermute | solution.py:89
  172.8 253.8 %copy-start.3 = (f32[1,256,1024]{1,2,0:T(8,128)S(1)}, f32[1,256,1024]{1,2,0:T(8,128)}, u32[]{:S(2)}) copy-start(f32[1,256,1024]{1,2,0:T(8,128)} %get-tuple-element.675) | copy-start | bytes 3145732
  172.8 4.3 collective-permute-start.1
  177.2 10.5 %collective-permute-start.1 = (bf16[1024,256]{1,0:T(8,128)(2,1)S(1)}, bf16[1024,256]{1,0:T(8,128)(2,1)}, u32[]{:S(2)}, u32[]{:S(2)}) collective-permute-start(bf16[1024,256]{1,0:T(8,128)(2,1)S(1)} %get-tuple-element.796), channel_id=1, source_target_pairs={{0,1},{1,2},{2,3},{4,5},{5,6},{6,7},{8,9},{9,10},{10,11},{12,13},{... | collective-permute-start | bytes 1572872 | tf_op jit(solution)/shard_map/while/body/eval_jaxpr/ppermute | solution.py:134
  187.8 16.4 %collective-permute-start.1 = (bf16[1024,256]{1,0:T(8,128)(2,1)S(1)}, bf16[1024,256]{1,0:T(8,128)(2,1)}, u32[]{:S(2)}, u32[]{:S(2)}) collective-permute-start(bf16[1024,256]{1,0:T(8,128)(2,1)S(1)} %get-tuple-element.796), channel_id=1, source_target_pairs={{0,1},{1,2},{2,3},{4,5},{5,6},{6,7},{8,9},{9,10},{10,11},{12,13},{... | collective-permute-start | bytes 1572872 | tf_op jit(solution)/shard_map/while/body/eval_jaxpr/ppermute | solution.py:134
  208.5 10.4 %collective-permute-start.1 = (bf16[1024,256]{1,0:T(8,128)(2,1)S(1)}, bf16[1024,256]{1,0:T(8,128)(2,1)}, u32[]{:S(2)}, u32[]{:S(2)}) collective-permute-start(bf16[1024,256]{1,0:T(8,128)(2,1)S(1)} %get-tuple-element.796), channel_id=1, source_target_pairs={{0,1},{1,2},{2,3},{4,5},{5,6},{6,7},{8,9},{9,10},{10,11},{12,13},{... | collective-permute-start | bytes 1572872 | tf_op jit(solution)/shard_map/while/body/eval_jaxpr/ppermute | solution.py:134
  223.1 10.5 %collective-permute-start.1 = (bf16[1024,256]{1,0:T(8,128)(2,1)S(1)}, bf16[1024,256]{1,0:T(8,128)(2,1)}, u32[]{:S(2)}, u32[]{:S(2)}) collective-permute-start(bf16[1024,256]{1,0:T(8,128)(2,1)S(1)} %get-tuple-element.796), channel_id=1, source_target_pairs={{0,1},{1,2},{2,3},{4,5},{5,6},{6,7},{8,9},{9,10},{10,11},{12,13},{... | collective-permute-start | bytes 1572872 | tf_op jit(solution)/shard_map/while/body/eval_jaxpr/ppermute | solution.py:134
  237.7 10.5 %collective-permute-start.1 = (bf16[1024,256]{1,0:T(8,128)(2,1)S(1)}, bf16[1024,256]{1,0:T(8,128)(2,1)}, u32[]{:S(2)}, u32[]{:S(2)}) collective-permute-start(bf16[1024,256]{1,0:T(8,128)(2,1)S(1)} %get-tuple-element.796), channel_id=1, source_target_pairs={{0,1},{1,2},{2,3},{4,5},{5,6},{6,7},{8,9},{9,10},{10,11},{12,13},{... | collective-permute-start | bytes 1572872 | tf_op jit(solution)/shard_map/while/body/eval_jaxpr/ppermute | solution.py:134
  252.3 10.5 %collective-permute-start.1 = (bf16[1024,256]{1,0:T(8,128)(2,1)S(1)}, bf16[1024,256]{1,0:T(8,128)(2,1)}, u32[]{:S(2)}, u32[]{:S(2)}) collective-permute-start(bf16[1024,256]{1,0:T(8,128)(2,1)S(1)} %get-tuple-element.796), channel_id=1, source_target_pairs={{0,1},{1,2},{2,3},{4,5},{5,6},{6,7},{8,9},{9,10},{10,11},{12,13},{... | collective-permute-start | bytes 1572872 | tf_op jit(solution)/shard_map/while/body/eval_jaxpr/ppermute | solution.py:134
  267.0 10.5 %collective-permute-start.1 = (bf16[1024,256]{1,0:T(8,128)(2,1)S(1)}, bf16[1024,256]{1,0:T(8,128)(2,1)}, u32[]{:S(2)}, u32[]{:S(2)}) collective-permute-start(bf16[1024,256]{1,0:T(8,128)(2,1)S(1)} %get-tuple-element.796), channel_id=1, source_target_pairs={{0,1},{1,2},{2,3},{4,5},{5,6},{6,7},{8,9},{9,10},{10,11},{12,13},{... | collective-permute-start | bytes 1572872 | tf_op jit(solution)/shard_map/while/body/eval_jaxpr/ppermute | solution.py:134
  281.6 10.5 %collective-permute-start.1 = (bf16[1024,256]{1,0:T(8,128)(2,1)S(1)}, bf16[1024,256]{1,0:T(8,128)(2,1)}, u32[]{:S(2)}, u32[]{:S(2)}) collective-permute-start(bf16[1024,256]{1,0:T(8,128)(2,1)S(1)} %get-tuple-element.796), channel_id=1, source_target_pairs={{0,1},{1,2},{2,3},{4,5},{5,6},{6,7},{8,9},{9,10},{10,11},{12,13},{... | collective-permute-start | bytes 1572872 | tf_op jit(solution)/shard_map/while/body/eval_jaxpr/ppermute | solution.py:134
  296.3 10.5 %collective-permute-start.1 = (bf16[1024,256]{1,0:T(8,128)(2,1)S(1)}, bf16[1024,256]{1,0:T(8,128)(2,1)}, u32[]{:S(2)}, u32[]{:S(2)}) collective-permute-start(bf16[1024,256]{1,0:T(8,128)(2,1)S(1)} %get-tuple-element.796), channel_id=1, source_target_pairs={{0,1},{1,2},{2,3},{4,5},{5,6},{6,7},{8,9},{9,10},{10,11},{12,13},{... | collective-permute-start | bytes 1572872 | tf_op jit(solution)/shard_map/while/body/eval_jaxpr/ppermute | solution.py:134
  310.9 10.5 %collective-permute-start.1 = (bf16[1024,256]{1,0:T(8,128)(2,1)S(1)}, bf16[1024,256]{1,0:T(8,128)(2,1)}, u32[]{:S(2)}, u32[]{:S(2)}) collective-permute-start(bf16[1024,256]{1,0:T(8,128)(2,1)S(1)} %get-tuple-element.796), channel_id=1, source_target_pairs={{0,1},{1,2},{2,3},{4,5},{5,6},{6,7},{8,9},{9,10},{10,11},{12,13},{... | collective-permute-start | bytes 1572872 | tf_op jit(solution)/shard_map/while/body/eval_jaxpr/ppermute | solution.py:134
  325.6 10.5 %collective-permute-start.1 = (bf16[1024,256]{1,0:T(8,128)(2,1)S(1)}, bf16[1024,256]{1,0:T(8,128)(2,1)}, u32[]{:S(2)}, u32[]{:S(2)}) collective-permute-start(bf16[1024,256]{1,0:T(8,128)(2,1)S(1)} %get-tuple-element.796), channel_id=1, source_target_pairs={{0,1},{1,2},{2,3},{4,5},{5,6},{6,7},{8,9},{9,10},{10,11},{12,13},{... | collective-permute-start | bytes 1572872 | tf_op jit(solution)/shard_map/while/body/eval_jaxpr/ppermute | solution.py:134
  340.3 10.5 %collective-permute-start.1 = (bf16[1024,256]{1,0:T(8,128)(2,1)S(1)}, bf16[1024,256]{1,0:T(8,128)(2,1)}, u32[]{:S(2)}, u32[]{:S(2)}) collective-permute-start(bf16[1024,256]{1,0:T(8,128)(2,1)S(1)} %get-tuple-element.796), channel_id=1, source_target_pairs={{0,1},{1,2},{2,3},{4,5},{5,6},{6,7},{8,9},{9,10},{10,11},{12,13},{... | collective-permute-start | bytes 1572872 | tf_op jit(solution)/shard_map/while/body/eval_jaxpr/ppermute | solution.py:134
  354.9 10.5 %collective-permute-start.1 = (bf16[1024,256]{1,0:T(8,128)(2,1)S(1)}, bf16[1024,256]{1,0:T(8,128)(2,1)}, u32[]{:S(2)}, u32[]{:S(2)}) collective-permute-start(bf16[1024,256]{1,0:T(8,128)(2,1)S(1)} %get-tuple-element.796), channel_id=1, source_target_pairs={{0,1},{1,2},{2,3},{4,5},{5,6},{6,7},{8,9},{9,10},{10,11},{12,13},{... | collective-permute-start | bytes 1572872 | tf_op jit(solution)/shard_map/while/body/eval_jaxpr/ppermute | solution.py:134
  369.6 10.5 %collective-permute-start.1 = (bf16[1024,256]{1,0:T(8,128)(2,1)S(1)}, bf16[1024,256]{1,0:T(8,128)(2,1)}, u32[]{:S(2)}, u32[]{:S(2)}) collective-permute-start(bf16[1024,256]{1,0:T(8,128)(2,1)S(1)} %get-tuple-element.796), channel_id=1, source_target_pairs={{0,1},{1,2},{2,3},{4,5},{5,6},{6,7},{8,9},{9,10},{10,11},{12,13},{... | collective-permute-start | bytes 1572872 | tf_op jit(solution)/shard_map/while/body/eval_jaxpr/ppermute | solution.py:134
  384.2 10.5 %collective-permute-start.1 = (bf16[1024,256]{1,0:T(8,128)(2,1)S(1)}, bf16[1024,256]{1,0:T(8,128)(2,1)}, u32[]{:S(2)}, u32[]{:S(2)}) collective-permute-start(bf16[1024,256]{1,0:T(8,128)(2,1)S(1)} %get-tuple-element.796), channel_id=1, source_target_pairs={{0,1},{1,2},{2,3},{4,5},{5,6},{6,7},{8,9},{9,10},{10,11},{12,13},{... | collective-permute-start | bytes 1572872 | tf_op jit(solution)/shard_map/while/body/eval_jaxpr/ppermute | solution.py:134
  398.9 10.5 %collective-permute-start.1 = (bf16[1024,256]{1,0:T(8,128)(2,1)S(1)}, bf16[1024,256]{1,0:T(8,128)(2,1)}, u32[]{:S(2)}, u32[]{:S(2)}) collective-permute-start(bf16[1024,256]{1,0:T(8,128)(2,1)S(1)} %get-tuple-element.796), channel_id=1, source_target_pairs={{0,1},{1,2},{2,3},{4,5},{5,6},{6,7},{8,9},{9,10},{10,11},{12,13},{... | collective-permute-start | bytes 1572872 | tf_op jit(solution)/shard_map/while/body/eval_jaxpr/ppermute | solution.py:134
  413.5 10.5 %collective-permute-start.1 = (bf16[1024,256]{1,0:T(8,128)(2,1)S(1)}, bf16[1024,256]{1,0:T(8,128)(2,1)}, u32[]{:S(2)}, u32[]{:S(2)}) collective-permute-start(bf16[1024,256]{1,0:T(8,128)(2,1)S(1)} %get-tuple-element.796), channel_id=1, source_target_pairs={{0,1},{1,2},{2,3},{4,5},{5,6},{6,7},{8,9},{9,10},{10,11},{12,13},{... | collective-permute-start | bytes 1572872 | tf_op jit(solution)/shard_map/while/body/eval_jaxpr/ppermute | solution.py:134
  (14 other events, 60.7 us)
Sparse Core Ops, SparseCore 0:
  61.5 82.4 all-reduce.2
where the time goes:
time: 444 us; the launch traced here: 440 us
  waiting for transfers between devices  247 us (56%)
  matrix products  83.1 us (19%)
  starting transfers between devices  45.4 us (10%)
  local copies, waits for them, and re-layouts  26.1 us (6%)
  between operations  17.5 us (4%)
  other arithmetic  13.9 us (3%)
  blocking collectives  6.64 us (1%)
    ppermute x18, waiting for transfers between devices, fwd_tick(): return (lax.ppermute(rows_out, 'stage', up_pairs), stage_outs)  165 us
    psum x1, waiting for transfers between devices, local_step(): lax.psum(grad_up[0, 0] + mat_tn(stage_in, dpre_own), 'data') / n_reps  77.4 us
    dot_general x16, matrix products, stage_forward(): jnp.dot(hidden, down_bf, preferred_element_type=jnp.float32)  66.6 us
    ppermute x18, starting transfers between devices, fwd_tick(): return (lax.ppermute(rows_out, 'stage', up_pairs), stage_outs)  23.2 us
    ppermute x3, starting transfers between devices, back_tick(): lax.ppermute(d_rows, 'stage', down_pairs)  22.2 us
    unnamed x31, local copies, waits for them, and re-layouts  13.3 us
  transfers between devices with their start and end apart: 22, of which 22 were waited for; matrix products, arithmetic and copies ran while one was open for 1% of the time, Pallas kernels for 0%

commit v1 on v0

v1 whole, which is shorter than its diff:
```python
import functools

import jax
import jax.numpy as jnp
from jax import lax
from jax.experimental import pallas as pl
from jax.experimental.pallas import tpu as pltpu
from jax.sharding import PartitionSpec as P

BETA1 = 0.9
BETA2 = 0.95
ADAM_EPS = 1e-8
WEIGHT_DECAY = 0.1
NORM_EPS = 1e-6
ADAM_STEP = 8
SQRT_TWO_PI = 0.7978845608028654
GELU_CUBIC = 0.044715

N_SENT = 6
MESH = pl.DeviceIdType.MESH
BF16 = jnp.bfloat16
F32 = jnp.float32


def tanh_part(pre_act):
    return jnp.tanh(SQRT_TWO_PI * (pre_act + GELU_CUBIC * pre_act * pre_act * pre_act))


def gelu_pair(pre_act):
    tanh_val = tanh_part(pre_act)
    act_value = 0.5 * pre_act * (1.0 + tanh_val)
    act_slope = 0.5 * (1.0 + tanh_val) + 0.5 * pre_act * (1.0 - tanh_val * tanh_val) * SQRT_TWO_PI * (1.0 + 3.0 * GELU_CUBIC * pre_act * pre_act)
    return act_value, act_slope


def mat_tn(left, right):
    return lax.dot_general(left, right, (((0,), (0,)), ((), ())), preferred_element_type=F32)


def mat_nt(left, right):
    return lax.dot_general(left, right, (((1,), (1,)), ((), ())), preferred_element_type=F32)


def adamw_update(master, first_mom, second_mom, grad_avg, clip_scale, learn_rate):
    scaled = clip_scale * grad_avg
    new_first = BETA1 * first_mom + (1.0 - BETA1) * scaled
    new_second = BETA2 * second_mom + (1.0 - BETA2) * scaled * scaled
    first_hat = new_first / (1.0 - BETA1 ** ADAM_STEP)
    second_hat = new_second / (1.0 - BETA2 ** ADAM_STEP)
    new_master = master - learn_rate * (first_hat / (jnp.sqrt(second_hat) + ADAM_EPS) + WEIGHT_DECAY * master)
    return new_master, new_first, new_second


def gelu_of_half(half):
    t = jnp.tanh(half * (2.0 * SQRT_TWO_PI + (8.0 * SQRT_TWO_PI * GELU_CUBIC) * (half * half)))
    return half + half * t


def stage_rows(src, up_half, down, dst):
    x = src[...]
    half = jnp.dot(x, up_half[...], preferred_element_type=F32)
    hidden = gelu_of_half(half).astype(BF16)
    y = jnp.dot(hidden, down[...], preferred_element_type=F32)
    dst[...] = (x.astype(F32) + y).astype(BF16)


def forward_part(stage, nb_hbm, up_own, down_own, up_aux, down_aux, out_hbm, nbuf, xin, yout, nb_sem, out_sem, send_sem, recv_sem):
    n_micro = nbuf.shape[0]
    n_kept = n_micro - N_SENT

    def load(i):
        return pltpu.make_async_copy(nb_hbm.at[i], nbuf.at[i], nb_sem.at[i])

    def store(i):
        return pltpu.make_async_copy(yout.at[i], out_hbm.at[i], out_sem.at[i])

    def push(src, i, peer):
        return pltpu.make_async_remote_copy(src_ref=src.at[i], dst_ref=xin.at[i], send_sem=send_sem.at[i], recv_sem=recv_sem.at[i], device_id={"stage": peer}, device_id_type=MESH)

    def arrived(i):
        push(yout, i, stage).wait_recv()

    def rotated(j):
        return lax.rem(j + n_kept, n_micro)

    def mixed(k):
        before = lax.div(k * N_SENT, n_micro)
        is_sent = lax.div((k + 1) * N_SENT, n_micro) - before
        return is_sent, is_sent * (n_kept + before) + (1 - is_sent) * (k - before)

    def finish_stores():
        def body(i, _):
            store(i).wait()
            return 0
        lax.fori_loop(0, n_micro, body, 0)

    def finish_sends(first, count):
        def body(i, _):
            push(yout, first + i, stage).wait_send()
            return 0
        lax.fori_loop(0, count, body, 0)

    @pl.when(stage == 0)
    def _():
        def start(j, _):
            load(rotated(j)).start()
            return 0
        lax.fori_loop(0, n_micro, start, 0)

        def body(j, _):
            i = rotated(j)
            load(i).wait()
            stage_rows(nbuf.at[i], up_own, down_own, yout.at[i])
            push(yout, i, 1).start()
            store(i).start()
            return 0
        lax.fori_loop(0, n_micro, body, 0)
        finish_sends(0, n_micro)
        finish_stores()

    @pl.when(stage == 1)
    def _():
        def body(j, _):
            i = rotated(j)
            arrived(i)
            stage_rows(xin.at[i], up_own, down_own, yout.at[i])

            @pl.when(j < N_SENT)
            def _():
                push(yout, i, 2).start()
            store(i).start()
            return 0
        lax.fori_loop(0, n_micro, body, 0)
        finish_sends(n_kept, N_SENT)
        finish_stores()

    @pl.when(stage == 2)
    def _():
        def body(k, _):
            is_sent, i = mixed(k)
            arrived(i)

            @pl.when(is_sent == 0)
            def _():
                stage_rows(xin.at[i], up_aux, down_aux, xin.at[i])
            stage_rows(xin.at[i], up_own, down_own, yout.at[i])
            push(yout, i, 3).start()
            store(i).start()
            return 0
        lax.fori_loop(0, n_micro, body, 0)
        finish_sends(0, n_micro)
        finish_stores()

    @pl.when(stage == 3)
    def _():
        def start(j, _):
            load(j).start()
            return 0
        lax.fori_loop(0, n_kept, start, 0)

        def first(j, _):
            load(j).wait()
            stage_rows(nbuf.at[j], up_aux, down_aux, nbuf.at[j])
            push(nbuf, j, 2).start()
            return 0
        lax.fori_loop(0, n_kept, first, 0)

        def body(k, _):
            _, i = mixed(k)
            arrived(i)
            stage_rows(xin.at[i], up_own, down_own, yout.at[i])
            store(i).start()
            return 0
        lax.fori_loop(0, n_micro, body, 0)
        finish_sends(0, n_kept)
        finish_stores()


def forward_kernel(nb_hbm, up_own, down_own, up_aux, down_aux, out_hbm, nbuf, xin, yout, nb_sem, out_sem, send_sem, recv_sem):
    stage = lax.axis_index("stage")
    barrier = pltpu.get_barrier_semaphore()

    @pl.when(stage > 0)
    def _():
        pl.semaphore_signal(barrier, inc=1, device_id={"stage": stage - 1}, device_id_type=MESH)

    @pl.when(stage < 3)
    def _():
        pl.semaphore_signal(barrier, inc=1, device_id={"stage": stage + 1}, device_id_type=MESH)

    pl.semaphore_wait(barrier, jnp.where((stage == 0) | (stage == 3), 1, 2))
    forward_part(stage, nb_hbm, up_own, down_own, up_aux, down_aux, out_hbm, nbuf, xin, yout, nb_sem, out_sem, send_sem, recv_sem)


def forward(next_batch, up_own, down_own, up_aux, down_aux):
    n_micro = next_batch.shape[0]
    vmem = pl.BlockSpec(memory_space=pltpu.VMEM)
    hbm = pl.BlockSpec(memory_space=pl.ANY)
    return pl.pallas_call(
        forward_kernel,
        name="forward_step",
        out_shape=jax.ShapeDtypeStruct(next_batch.shape, BF16),
        in_specs=[hbm, vmem, vmem, vmem, vmem],
        out_specs=hbm,
        scratch_shapes=[
            pltpu.VMEM(next_batch.shape, BF16),
            pltpu.VMEM(next_batch.shape, BF16),
            pltpu.VMEM(next_batch.shape, BF16),
            pltpu.SemaphoreType.DMA((n_micro,)),
            pltpu.SemaphoreType.DMA((n_micro,)),
            pltpu.SemaphoreType.DMA((n_micro,)),
            pltpu.SemaphoreType.DMA((n_micro,)),
        ],
        compiler_params=pltpu.CompilerParams(collective_id=1, has_side_effects=True, vmem_limit_bytes=60 * 1024 * 1024),
    )(next_batch, up_own, down_own, up_aux, down_aux)


def solution(mesh):
    n_stages = mesh.shape['stage']
    n_reps = mesh.shape['data']
    last_stage = n_stages - 1
    down_pairs = [(source, source - 1) for source in range(1, n_stages)]

    def local_step(master_up, master_down, mom1_up, mom1_down, mom2_up, mom2_down, grad_up, grad_down, stage_acts, loss_grad, next_batch, learn_rate, max_norm):
        stage_idx = lax.axis_index('stage')
        stage_in = stage_acts[0]
        up_bf = master_up[0].astype(BF16)
        down_bf = master_down[0].astype(BF16)

        pre_act = jnp.dot(stage_in, up_bf, preferred_element_type=F32)
        act_value, act_slope = gelu_pair(pre_act)
        hidden = act_value.astype(BF16)

        grad_in = loss_grad
        for step_idx in range(n_stages):
            d_pre = (mat_nt(grad_in, down_bf) * act_slope).astype(BF16)
            if step_idx < last_stage:
                d_rows = (grad_in.astype(F32) + mat_nt(d_pre, up_bf)).astype(BF16)
                received = lax.ppermute(d_rows, 'stage', down_pairs)
                grad_in = jnp.where(stage_idx == last_stage - 1 - step_idx, received, grad_in)

        gbar_up = lax.psum(grad_up[0, 0] + mat_tn(stage_in, d_pre), 'data') / n_reps
        gbar_down = lax.psum(grad_down[0, 0] + mat_tn(hidden, grad_in), 'data') / n_reps
        local_sq = jnp.sum(gbar_up * gbar_up) + jnp.sum(gbar_down * gbar_down)
        grad_norm = jnp.sqrt(lax.psum(local_sq, 'stage'))
        clip_scale = jnp.minimum(1.0, max_norm / (grad_norm + NORM_EPS))
        new_up, new_m1_up, new_m2_up = adamw_update(master_up[0], mom1_up[0], mom2_up[0], gbar_up, clip_scale, learn_rate)
        new_down, new_m1_down, new_m2_down = adamw_update(master_down[0], mom1_down[0], mom2_down[0], gbar_down, clip_scale, learn_rate)
        up_half = new_up.astype(BF16) * jnp.asarray(0.5, BF16)
        down_new = new_down.astype(BF16)
        up_aux = lax.ppermute(up_half, 'stage', [(0, 3), (1, 2)])
        down_aux = lax.ppermute(down_new, 'stage', [(0, 3), (1, 2)])
        stage_outs = forward(next_batch, up_half, down_new, up_aux, down_aux)
        return (new_up[None], new_down[None], new_m1_up[None], new_m1_down[None], new_m2_up[None], new_m2_down[None], stage_outs[None])

    w_spec = P('stage', None, None)
    g_spec = P('data', 'stage', None, None)
    in_specs = (w_spec, w_spec, w_spec, w_spec, w_spec, w_spec, g_spec, g_spec, P('stage', 'data', None), P('data', None), P(None, 'data', None), P(), P())
    out_specs = (w_spec, w_spec, w_spec, w_spec, w_spec, w_spec, P('stage', None, 'data', None))
    return jax.shard_map(local_step, mesh=mesh, in_specs=in_specs, out_specs=out_specs, check_vma=False)
```

time: 444 us -> 247 us (0.56)
  waiting for transfers between devices: 247 us -> 94.4 us
  Pallas kernels: 0 us -> 49.4 us
  matrix products: 83.1 us -> 33.8 us
  starting transfers between devices: 45.4 us -> 22.2 us
  local copies, waits for them, and re-layouts: 26.1 us -> 8.4 us
    ppermute x21 -> x5, waiting for transfers between devices: 169 us -> 24.7 us  [the longest x1 11.2 us: local_step(): up_aux = lax.ppermute(up_half, 'stage', [(0, 3), (1, 2)])]
    dot_general x17 -> x1, matrix products: 72 us -> 3.95 us  [local_step(): pre_act = jnp.dot(stage_in, up_bf, preferred_element_type=F32)]
    pallas_call x0 -> x1, Pallas kernels: none -> 49.4 us  [forward(): pl.pallas_call(forward_kernel, name='forward_step', out_shape=jax.ShapeDt...]
    ppermute x21 -> x5, starting transfers between devices: 45.4 us -> 22.2 us  [the longest x3 19.6 us: local_step(): received = lax.ppermute(d_rows, 'stage', down_pairs)]
    dot_general x2 -> x3, matrix products: 5.47 us -> 18.3 us  [mat_nt(): lax.dot_general(left, right, (((1,), (1,)), ((), ())), preferred_element_...]
    psum x1, waiting for transfers between devices: 77.4 us -> 69.7 us  [local_step(): gbar_up = lax.psum(grad_up[0, 0] + mat_tn(stage_in, d_pre), 'data') / n_reps]
    broadcast_in_dim x3 -> x0, local copies, waits for them, and re-layouts: 7.38 us -> none  [the longest x1 4.21 us: local_step(): outs_init = jnp.zeros((n_micro, tok_rows, model_width), jnp.bfloat16)]
    dot_general x2, matrix products: 5.59 us -> 11.6 us  [mat_tn(): lax.dot_general(left, right, (((0,), (0,)), ((), ())), preferred_element_...]
  transfers between devices with their start and end apart: 22 -> 6, of which waited for: 22 -> 6; matrix products, arithmetic and copies ran while one was open for 1% -> 1% of each run, Pallas kernels for 0% -> 0%
where the time goes in v1:
time: 247 us
  waiting for transfers between devices  94.4 us (38%)
  Pallas kernels  49.4 us (20%)
  matrix products  33.8 us (14%)
  starting transfers between devices  22.2 us (9%)
  between operations  17.7 us (7%)
  other arithmetic  14.2 us (6%)
  local copies, waits for them, and re-layouts  8.4 us (3%)
  blocking collectives  6.46 us (3%)
    psum x1, waiting for transfers between devices, local_step(): gbar_up = lax.psum(grad_up[0, 0] + mat_tn(stage_in, d_pre), 'data') / n_reps  69.7 us
    pallas_call x1, Pallas kernels, forward(): pl.pallas_call(forward_kernel, name='forward_step', out_shape=jax.ShapeDt...  49.4 us
    ppermute x3, starting transfers between devices, local_step(): received = lax.ppermute(d_rows, 'stage', down_pairs)  19.6 us
    dot_general x3, matrix products, mat_nt(): lax.dot_general(left, right, (((1,), (1,)), ((), ())), preferred_element_...  18.3 us
    dot_general x2, matrix products, mat_tn(): lax.dot_general(left, right, (((0,), (0,)), ((), ())), preferred_element_...  11.6 us
    ppermute x1, waiting for transfers between devices, local_step(): up_aux = lax.ppermute(up_half, 'stage', [(0, 3), (1, 2)])  11.2 us
    ppermute x1, waiting for transfers between devices, local_step(): down_aux = lax.ppermute(down_new, 'stage', [(0, 3), (1, 2)])  9.99 us
    unnamed x29, local copies, waits for them, and re-layouts  8.4 us
  transfers between devices with their start and end apart: 6, of which 6 were waited for; matrix products, arithmetic and copies ran while one was open for 1% of the time, Pallas kernels for 0%

profile of v1, /device:TPU:3, one launch (start us, length us, event | category | flops | bytes accessed | tf_op | source)
XLA Modules:
  0.0 246.6 jit_solution(18364585105802611938)
XLA Ops:
  7.2 1.4 bitcast_convert_fusion
  8.7 4.0 %fusion.21 = f32[1024,1024]{1,0:T(8,128)} fusion(bf16[1,1024,256]{2,1,0:T(8,128)(2,1)S(1)} %copy-done, f32[1,256,1024]{2,1,0:T(8,128)} %param.13), kind=kOutput, calls=%fused_computation.42 | convolution fusion | flops 537133056 | bytes 5767168 | tf_op jit(solution)/shard_map/dot_general | solution.py:230
  12.6 6.0 %fusion.14 = bf16[1024,256]{1,0:T(8,128)(2,1)} fusion(bf16[1024,256]{1,0:T(8,128)(2,1)S(1)} %copy-done.11, bf16[1024,256]{1,0:T(8,128)(2,1)S(1)} %bitcast_convert_fusion, f32[1024,1024]{1,0:T(8,128)} %fusion.21, f32[1,256,1024]{2,1,0:T(8,128)S(1)} %copy-done.3), kind=kOutput, calls=%fused_computation.23 | convolution fusion | flops 1094451200 | bytes 6815744 | tf_op jit(solution)/shard_map/dot_general | solution.py:41
  18.6 2.6 %collective-permute-start = (bf16[1024,256]{1,0:T(8,128)(2,1)}, bf16[1024,256]{1,0:T(8,128)(2,1)S(1)}, u32[]{:S(2)}, u32[]{:S(2)}) collective-permute-start(bf16[1024,256]{1,0:T(8,128)(2,1)} %fusion.14), channel_id=1, source_target_pairs={{1,0},{2,1},{3,2},{5,4},{6,5},{7,6},{9,8},{10,9},{11,10},{13,12},{... | collective-permute-start | bytes 1572872 | tf_op jit(solution)/shard_map/ppermute | solution.py:239
  21.2 1.5 collective-permute-done
  22.7 6.0 %add_convert_fusion.1 = bf16[1024,256]{1,0:T(8,128)(2,1)} fusion(bf16[1024,256]{1,0:T(8,128)(2,1)S(1)} %bitcast_convert_fusion, bf16[1024,256]{1,0:T(8,128)(2,1)S(1)} %collective-permute-done, bf16[1024,256]{1,0:T(8,128)(2,1)S(1)} %copy-done.11, pred[]{:T(512)S(6)} %eq.11, f32[1024,1024]{1,0:T(8,128)} %fusion.21, f32[1,256,1024]{2,1,0:T(8,128)S(1)} %copy-done.3), kind=kOutput, calls=%fused_computation.41 | convolution fusion | flops 1094975488 | bytes 7340033 | tf_op jit(solution)/shard_map/dot_general | solution.py:41
  28.7 7.8 %collective-permute-start.1 = (bf16[1024,256]{1,0:T(8,128)(2,1)}, bf16[1024,256]{1,0:T(8,128)(2,1)}, u32[]{:S(2)}, u32[]{:S(2)}) collective-permute-start(bf16[1024,256]{1,0:T(8,128)(2,1)} %add_convert_fusion.1), channel_id=1, source_target_pairs={{1,0},{2,1},{3,2},{5,4},{6,5},{7,6},{9,8},{10,9},{11,10},{13,12},{... | collective-permute-start | bytes 1572872 | tf_op jit(solution)/shard_map/ppermute | solution.py:239
  38.2 6.3 %add_convert_fusion = bf16[1024,256]{1,0:T(8,128)(2,1)} fusion(bf16[1024,256]{1,0:T(8,128)(2,1)} %broadcast_select_fusion.1, bf16[1024,256]{1,0:T(8,128)(2,1)S(1)} %bitcast_convert_fusion, f32[1024,1024]{1,0:T(8,128)} %fusion.21, f32[1,256,1024]{2,1,0:T(8,128)S(1)} %copy-done.3), kind=kOutput, calls=%fused_computation.40 | convolution fusion | flops 1094451200 | bytes 6815744 | tf_op jit(solution)/shard_map/dot_general | solution.py:41
  44.5 9.2 %collective-permute-start.2 = (bf16[1024,256]{1,0:T(8,128)(2,1)}, bf16[1024,256]{1,0:T(8,128)(2,1)S(1)}, u32[]{:S(2)}, u32[]{:S(2)}) collective-permute-start(bf16[1024,256]{1,0:T(8,128)(2,1)} %add_convert_fusion), channel_id=1, source_target_pairs={{1,0},{2,1},{3,2},{5,4},{6,5},{7,6},{9,8},{10,9},{11,10},{13,12},{... | collective-permute-start | bytes 1572872 | tf_op jit(solution)/shard_map/ppermute | solution.py:239
  53.7 1.3 collective-permute-done.2
  54.9 5.0 %fusion.11 = f32[1024,256]{1,0:T(8,128)} fusion(f32[1024,1024]{1,0:T(8,128)} %fusion.21, f32[1,1,1024,256]{3,2,1,0:T(8,128)} %param.20, bf16[1024,256]{1,0:T(8,128)(2,1)S(1)} %collective-permute-done.2, bf16[1024,256]{1,0:T(8,128)(2,1)S(1)} %copy-done.12, pred[]{:T(512)S(6)} %eq.9), kind=kOutput, calls=%fused_computation.20 | convolution fusion | flops 546832384 | bytes 7340033 | tf_op jit(solution)/shard_map/dot_general | solution.py:37
  60.0 6.5 %fusion.12 = f32[256,1024]{1,0:T(8,128)} fusion(bf16[1024,256]{1,0:T(8,128)(2,1)S(1)} %bitcast_convert_fusion, f32[1,1,256,1024]{3,2,1,0:T(8,128)S(1)} %copy-done.13, bf16[1,1024,256]{2,1,0:T(8,128)(2,1)S(1)} %copy-done, bf16[1024,256]{1,0:T(8,128)(2,1)S(1)} %collective-permute-done.2, bf16[1024,256]{1,0:T(8,128)(2,1)S(1)} %copy-done.12, pred[]{:T(512)S(6)} %eq.9, ...), kind=kOutput, calls=%fused_computation.21 | convolution fusion | flops 1094189056 | bytes 8388609 | tf_op jit(solution)/shard_map/dot_general | solution.py:37
  67.3 69.7 %all-reduce.3.cloned.1.call-done = (f32[256,1024]{1,0:T(8,128)}, f32[1024,256]{1,0:T(8,128)}) async-done(((f32[256,1024]{1,0:T(8,128)}, f32[1024,256]{1,0:T(8,128)}), (f32[256,1024]{1,0:T(8,128)}, f32[1024,256]{1,0:T(8,128)})) %all-reduce.3.cloned.1.call-update) | async-done | bytes 2097168 | tf_op jit(solution)/shard_map/psum | solution.py:242
  136.9 2.1 multiply_reduce_fusion
  139.0 2.1 multiply_reduce_fusion.1
  143.2 6.5 %psum.23 = f32[]{:T(128)} all-reduce(f32[]{:T(128)S(6)} %add.79), channel_id=1, replica_groups=mesh['data'=4,'stage'=4] {'stage'}, use_global_device_ids=true, to_apply=%region_4.5 | all-reduce | flops 1 | bytes 8 | tf_op jit(solution)/shard_map/psum | solution.py:245
  150.4 4.2 %fusion.41 = (bf16[1024,256]{1,0:T(8,128)(2,1)S(1)}, f32[1024,256]{1,0:T(8,128)}, f32[1,1024,256]{2,1,0:T(8,128)}, f32[1,1024,256]{2,1,0:T(8,128)}) fusion(f32[1,1024,256]{2,1,0:T(8,128)} %param.18, f32[1024,256]{1,0:T(8,128)} %get-tuple-element.8, f32[]{:T(128)S(6)} %mul.187, f32[1,1024,256]{2,1,0:T(8,128)} %param.16, f32[]{:T(128)S(6)} %copy.25, ...), kind=kLoop, calls=%fused_computation.59 | loop fusion | flops 4456448 | bytes 7864328 | tf_op jit(solution)/shard_map/convert_element_type | solution.py:250
  154.6 1.3 collective-permute-start.4
  155.9 1.9 convert_multiply_fusion
  159.1 1.7 fusion.29
  160.8 10.0 %collective-permute-done.4.down_aux = bf16[1024,256]{1,0:T(8,128)(2,1)S(1)} collective-permute-done((bf16[1024,256]{1,0:T(8,128)(2,1)S(1)}, bf16[1024,256]{1,0:T(8,128)(2,1)S(1)}, u32[]{:S(2)}, u32[]{:S(2)}) %collective-permute-start.4) | collective-permute-done | bytes 524320 | tf_op jit(solution)/shard_map/ppermute | solution.py:252
  170.8 11.2 %collective-permute-done.3.up_aux = bf16[256,1024]{1,0:T(8,128)(2,1)S(1)} collective-permute-done((bf16[256,1024]{1,0:T(8,128)(2,1)S(1)}, bf16[256,1024]{1,0:T(8,128)(2,1)S(1)}, u32[]{:S(2)}, u32[]{:S(2)}) %collective-permute-start.3) | collective-permute-done | bytes 524320 | tf_op jit(solution)/shard_map/ppermute | solution.py:251
  182.8 49.4 %forward_step.1 = bf16[16,1024,256]{2,1,0:T(8,128)(2,1)} custom-call(bf16[16,1024,256]{2,1,0:T(8,128)(2,1)} %nb_hbm.1, bf16[256,1024]{1,0:T(8,128)(2,1)} %copy-done.8, bf16[1024,256]{1,0:T(8,128)(2,1)} %copy-done.7, bf16[256,1024]{1,0:T(8,128)(2,1)} %copy-done.10, bf16[1024,256]{1,0:T(8,128)(2,1)} %copy-done.9), custom_call_target="tpu_custom_call" | custom-call | tf_op jit(solution)/shard_map/forward_step/pallas_call | solution.py:199
  232.2 7.5 %copy.27 = bf16[1,16,1024,256]{3,2,1,0:T(8,128)(2,1)} copy(bf16[1,16,1024,256]{3,2,1,0:T(8,128)(2,1)} %bitcast.117) | data formatting | bytes 16777216
  (33 shorter events, 3.8 us)
Async XLA Ops:
  7.2 1.5 copy-start
  7.2 5.4 %copy-start.3 = (f32[1,256,1024]{2,1,0:T(8,128)S(1)}, f32[1,256,1024]{2,1,0:T(8,128)}, u32[]{:S(2)}) copy-start(f32[1,256,1024]{2,1,0:T(8,128)} %param.13) | copy-start | bytes 3145732
  7.2 5.4 %copy-start.11 = (bf16[1024,256]{1,0:T(8,128)(2,1)S(1)}, bf16[1024,256]{1,0:T(8,128)(2,1)}, u32[]{:S(2)}) copy-start(bf16[1024,256]{1,0:T(8,128)(2,1)} %param.22) | copy-start | bytes 1572868
  7.2 129.7 %all-reduce.3.cloned.1.call-start = ((), (), s32[]{:S(2)}) async-start(), calls=%async_computation | async-start | bytes 4194304 | tf_op jit(solution)/shard_map/psum | solution.py:242
  18.6 4.1 %collective-permute-start = (bf16[1024,256]{1,0:T(8,128)(2,1)}, bf16[1024,256]{1,0:T(8,128)(2,1)S(1)}, u32[]{:S(2)}, u32[]{:S(2)}) collective-permute-start(bf16[1024,256]{1,0:T(8,128)(2,1)} %fusion.14), channel_id=1, source_target_pairs={{1,0},{2,1},{3,2},{5,4},{6,5},{7,6},{9,8},{10,9},{11,10},{13,12},{... | collective-permute-start | bytes 1572872 | tf_op jit(solution)/shard_map/ppermute | solution.py:239
  28.7 8.6 %collective-permute-start.1 = (bf16[1024,256]{1,0:T(8,128)(2,1)}, bf16[1024,256]{1,0:T(8,128)(2,1)}, u32[]{:S(2)}, u32[]{:S(2)}) collective-permute-start(bf16[1024,256]{1,0:T(8,128)(2,1)} %add_convert_fusion.1), channel_id=1, source_target_pairs={{1,0},{2,1},{3,2},{5,4},{6,5},{7,6},{9,8},{10,9},{11,10},{13,12},{... | collective-permute-start | bytes 1572872 | tf_op jit(solution)/shard_map/ppermute | solution.py:239
  38.2 16.8 %copy-start.12 = (bf16[1024,256]{1,0:T(8,128)(2,1)S(1)}, bf16[1024,256]{1,0:T(8,128)(2,1)}, u32[]{:S(2)}) copy-start(bf16[1024,256]{1,0:T(8,128)(2,1)} %broadcast_select_fusion.1) | copy-start | bytes 1572868
  44.5 10.5 %collective-permute-start.2 = (bf16[1024,256]{1,0:T(8,128)(2,1)}, bf16[1024,256]{1,0:T(8,128)(2,1)S(1)}, u32[]{:S(2)}, u32[]{:S(2)}) collective-permute-start(bf16[1024,256]{1,0:T(8,128)(2,1)} %add_convert_fusion), channel_id=1, source_target_pairs={{1,0},{2,1},{3,2},{5,4},{6,5},{7,6},{9,8},{10,9},{11,10},{13,12},{... | collective-permute-start | bytes 1572872 | tf_op jit(solution)/shard_map/ppermute | solution.py:239
  53.6 6.3 %copy-start.13 = (f32[1,1,256,1024]{3,2,1,0:T(8,128)S(1)}, f32[1,1,256,1024]{3,2,1,0:T(8,128)}, u32[]{:S(2)}) copy-start(f32[1,1,256,1024]{3,2,1,0:T(8,128)} %param.19) | copy-start | bytes 3145732
  66.5 83.9 %copy-start.2 = (f32[1,1024,256]{2,1,0:T(8,128)S(1)}, f32[1,1024,256]{2,1,0:T(8,128)}, u32[]{:S(2)}) copy-start(f32[1,1024,256]{2,1,0:T(8,128)} %param.14) | copy-start | bytes 3145732
  141.1 14.8 %copy-start.1 = (f32[256,1024]{1,0:T(8,128)S(1)}, f32[256,1024]{1,0:T(8,128)}, u32[]{:S(2)}) copy-start(f32[256,1024]{1,0:T(8,128)} %get-tuple-element.7) | copy-start | bytes 3145732
  150.4 5.5 %copy-start.4 = (f32[1,256,1024]{2,1,0:T(8,128)S(1)}, f32[1,256,1024]{2,1,0:T(8,128)}, u32[]{:S(2)}) copy-start(f32[1,256,1024]{2,1,0:T(8,128)} %param.13) | copy-start | bytes 3145732
  150.4 5.5 %copy-start.5 = (f32[1,256,1024]{2,1,0:T(8,128)S(1)}, f32[1,256,1024]{2,1,0:T(8,128)}, u32[]{:S(2)}) copy-start(f32[1,256,1024]{2,1,0:T(8,128)} %param.17) | copy-start | bytes 3145732
  150.4 5.5 %copy-start.6 = (f32[1,256,1024]{2,1,0:T(8,128)S(1)}, f32[1,256,1024]{2,1,0:T(8,128)}, u32[]{:S(2)}) copy-start(f32[1,256,1024]{2,1,0:T(8,128)} %param.15) | copy-start | bytes 3145732
  154.6 6.2 %copy-start.7 = (bf16[1024,256]{1,0:T(8,128)(2,1)}, bf16[1024,256]{1,0:T(8,128)(2,1)S(1)}, u32[]{:S(2)}) copy-start(bf16[1024,256]{1,0:T(8,128)(2,1)S(1)} %get-tuple-element.9.down_own) | copy-start | bytes 1572868
  154.6 16.2 %collective-permute-start.4 = (bf16[1024,256]{1,0:T(8,128)(2,1)S(1)}, bf16[1024,256]{1,0:T(8,128)(2,1)S(1)}, u32[]{:S(2)}, u32[]{:S(2)}) collective-permute-start(bf16[1024,256]{1,0:T(8,128)(2,1)S(1)} %get-tuple-element.9.down_own), channel_id=1, source_target_pairs={{0,3},{1,2},{4,7},{5,6},{8,11},{9,10},{12,15},{13,14}} | collective-permute-start | bytes 1572872 | tf_op jit(solution)/shard_map/ppermute | solution.py:252
  157.8 24.2 %copy-start.8 = (bf16[256,1024]{1,0:T(8,128)(2,1)}, bf16[256,1024]{1,0:T(8,128)(2,1)S(1)}, u32[]{:S(2)}) copy-start(bf16[256,1024]{1,0:T(8,128)(2,1)S(1)} %get-tuple-element.11.up_own) | copy-start | bytes 1572868
  157.8 24.2 %collective-permute-start.3 = (bf16[256,1024]{1,0:T(8,128)(2,1)S(1)}, bf16[256,1024]{1,0:T(8,128)(2,1)S(1)}, u32[]{:S(2)}, u32[]{:S(2)}) collective-permute-start(bf16[256,1024]{1,0:T(8,128)(2,1)S(1)} %get-tuple-element.11.up_own), channel_id=1, source_target_pairs={{0,3},{1,2},{4,7},{5,6},{8,11},{9,10},{12,15},{13,14}} | collective-permute-start | bytes 1572872 | tf_op jit(solution)/shard_map/ppermute | solution.py:251
  170.8 11.2 %copy-start.9 = (bf16[1024,256]{1,0:T(8,128)(2,1)}, bf16[1024,256]{1,0:T(8,128)(2,1)S(1)}, u32[]{:S(2)}) copy-start(bf16[1024,256]{1,0:T(8,128)(2,1)S(1)} %collective-permute-done.4.down_aux) | copy-start | bytes 1572868
  182.0 0.8 copy-start.10
Sparse Core Ops, SparseCore 0:
  66.6 70.2 all-reduce.2

commit v2 on v1

v2 whole, which is shorter than its diff:
```python
import jax
import jax.numpy as jnp
from jax import lax
from jax.experimental import pallas as pl
from jax.experimental.pallas import tpu as pltpu
from jax.sharding import PartitionSpec as P

BETA1 = 0.9
BETA2 = 0.95
ADAM_EPS = 1e-8
WEIGHT_DECAY = 0.1
NORM_EPS = 1e-6
ADAM_STEP = 8
SQRT_TWO_PI = 0.7978845608028654
GELU_CUBIC = 0.044715

N_SENT = 6
N_CHUNK = 4
MESH = pl.DeviceIdType.MESH
BF16 = jnp.bfloat16
F32 = jnp.float32


def mat_tn(left, right):
    return lax.dot_general(left, right, (((0,), (0,)), ((), ())), preferred_element_type=F32)


def mat_nt(left, right):
    return lax.dot_general(left, right, (((1,), (1,)), ((), ())), preferred_element_type=F32)


def adamw_update(master, first_mom, second_mom, grad_avg, clip_scale, learn_rate):
    scaled = clip_scale * grad_avg
    new_first = BETA1 * first_mom + (1.0 - BETA1) * scaled
    new_second = BETA2 * second_mom + (1.0 - BETA2) * scaled * scaled
    first_hat = new_first / (1.0 - BETA1 ** ADAM_STEP)
    second_hat = new_second / (1.0 - BETA2 ** ADAM_STEP)
    new_master = master - learn_rate * (first_hat / (jnp.sqrt(second_hat) + ADAM_EPS) + WEIGHT_DECAY * master)
    return new_master, new_first, new_second


def gelu_of_half(half):
    t = jnp.tanh(half * (2.0 * SQRT_TWO_PI + (8.0 * SQRT_TWO_PI * GELU_CUBIC) * (half * half)))
    return half + half * t


def stage_rows(src, up_half, down, dst):
    x = src[...]
    half = jnp.dot(x, up_half[...], preferred_element_type=F32)
    hidden = gelu_of_half(half).astype(BF16)
    y = jnp.dot(hidden, down[...], preferred_element_type=F32)
    dst[...] = (x.astype(F32) + y).astype(BF16)


def forward_part(stage, own_ready, aux_ready, relay_mean, nb_hbm, up_own, down_own, up_aux, down_aux, out_hbm, nbuf, xin, yout, nb_sem, out_sem, send_sem, recv_sem):
    n_micro = nbuf.shape[0]
    n_kept = n_micro - N_SENT

    def load(i):
        return pltpu.make_async_copy(nb_hbm.at[i], nbuf.at[i], nb_sem.at[i])

    def store(i):
        return pltpu.make_async_copy(yout.at[i], out_hbm.at[i], out_sem.at[i])

    def push(src, i, peer):
        return pltpu.make_async_remote_copy(src_ref=src.at[i], dst_ref=xin.at[i], send_sem=send_sem.at[i], recv_sem=recv_sem.at[i], device_id={"stage": peer}, device_id_type=MESH)

    def arrived(i):
        push(yout, i, stage).wait_recv()

    def rotated(j):
        return lax.rem(j + n_kept, n_micro)

    def mixed(k):
        before = lax.div(k * N_SENT, n_micro)
        is_sent = lax.div((k + 1) * N_SENT, n_micro) - before
        return is_sent, is_sent * (n_kept + before) + (1 - is_sent) * (k - before)

    def finish_stores():
        def body(i, _):
            store(i).wait()
            return 0
        lax.fori_loop(0, n_micro, body, 0)

    def finish_sends(first, count):
        def body(i, _):
            push(yout, first + i, stage).wait_send()
            return 0
        lax.fori_loop(0, count, body, 0)

    @pl.when(stage == 0)
    def _():
        own_ready()

        def body(j, _):
            i = rotated(j)
            load(i).wait()
            stage_rows(nbuf.at[i], up_own, down_own, yout.at[i])
            push(yout, i, 1).start()
            store(i).start()
            relay_mean(j == 7)
            return 0
        lax.fori_loop(0, n_micro, body, 0)
        finish_sends(0, n_micro)
        finish_stores()

    @pl.when(stage == 1)
    def _():
        own_ready()

        def body(j, _):
            i = rotated(j)
            arrived(i)
            stage_rows(xin.at[i], up_own, down_own, yout.at[i])

            @pl.when(j < N_SENT)
            def _():
                push(yout, i, 2).start()
            store(i).start()
            relay_mean(j == 7)
            return 0
        lax.fori_loop(0, n_micro, body, 0)
        finish_sends(n_kept, N_SENT)
        finish_stores()

    @pl.when(stage == 2)
    def _():
        aux_ready()
        own_ready()

        def body(k, _):
            is_sent, i = mixed(k)
            arrived(i)

            @pl.when(is_sent == 0)
            def _():
                stage_rows(xin.at[i], up_aux, down_aux, xin.at[i])
            stage_rows(xin.at[i], up_own, down_own, yout.at[i])
            push(yout, i, 3).start()
            store(i).start()
            relay_mean(k == 6)
            return 0
        lax.fori_loop(0, n_micro, body, 0)
        finish_sends(0, n_micro)
        finish_stores()

    @pl.when(stage == 3)
    def _():
        aux_ready()

        def first(j, _):
            load(j).wait()
            stage_rows(nbuf.at[j], up_aux, down_aux, nbuf.at[j])
            push(nbuf, j, 2).start()
            return 0
        lax.fori_loop(0, n_kept, first, 0)
        own_ready()

        def body(k, _):
            _, i = mixed(k)
            arrived(i)
            stage_rows(xin.at[i], up_own, down_own, yout.at[i])
            store(i).start()
            relay_mean(k == 1)
            return 0
        lax.fori_loop(0, n_micro, body, 0)
        finish_sends(0, n_kept)
        finish_stores()


def start_loads(stage, nb_hbm, nbuf, nb_sem):
    n_micro = nbuf.shape[0]
    n_kept = n_micro - N_SENT

    def body(j, _):
        i = lax.rem(j + n_kept, n_micro)
        pltpu.make_async_copy(nb_hbm.at[i], nbuf.at[i], nb_sem.at[i]).start()
        return 0

    @pl.when(stage == 0)
    def _():
        lax.fori_loop(0, n_micro, body, 0)

    @pl.when(stage == 3)
    def _():
        lax.fori_loop(N_SENT, n_micro, body, 0)


def step_kernel(up_hbm, down_hbm, m1_up_hbm, m1_down_hbm, m2_up_hbm, m2_down_hbm, gu_hbm, gv_hbm, acts_hbm, loss_hbm, nb_hbm, rate_ref, norm_ref,
                out_hbm, mean_up_hbm, mean_down_hbm, clip_out,
                up32, down32, gu, gv, mean_up, mean_down, acts, gbuf, dxbuf, hid, slope, dpre, up_bf, down_bf,
                ru1, rv1, ru2, rv2, mq_up, mq_down, up_own, down_own, up_aux, down_aux, sq_all, nbuf, xin, yout,
                in_sem, g_send, g_recv, rs_send, rs_recv, sq_send, sq_recv, ag_send, ag_recv, aux_send, aux_recv,
                nb_sem, out_sem, send_sem, recv_sem):
    stage = lax.axis_index("stage")
    data = lax.axis_index("data")
    z = lax.div(data, 2)
    y = lax.rem(data, 2)
    me = data * 4 + stage
    z_peer = 2 * (1 - z) + y
    y_peer = 2 * z + (1 - y)
    n_tok = acts.shape[0]
    chunk = n_tok // N_CHUNK

    def up_rows(zz, yy, first=0, count=64):
        return pl.ds(pl.multiple_of(128 * yy + 64 * zz + first, 32), count)

    def down_rows(zz, yy, first=0, count=256):
        return pl.ds(pl.multiple_of(512 * zz + 256 * yy + first, 128), count)

    own_up, own_down = up_rows(z, y), down_rows(z, y)
    loads = [
        pltpu.make_async_copy(acts_hbm, acts, in_sem.at[0]),
        pltpu.make_async_copy(up_hbm, up32, in_sem.at[1]),
        pltpu.make_async_copy(down_hbm, down32, in_sem.at[2]),
        pltpu.make_async_copy(gv_hbm, gv, in_sem.at[3]),
        pltpu.make_async_copy(gu_hbm, gu, in_sem.at[4]),
        pltpu.make_async_copy(m1_up_hbm.at[own_up], mq_up.at[0], in_sem.at[5]),
        pltpu.make_async_copy(m2_up_hbm.at[own_up], mq_up.at[1], in_sem.at[6]),
        pltpu.make_async_copy(m1_down_hbm.at[own_down], mq_down.at[0], in_sem.at[7]),
        pltpu.make_async_copy(m2_down_hbm.at[own_down], mq_down.at[1], in_sem.at[8]),
    ]
    load_loss = pltpu.make_async_copy(loss_hbm, gbuf, in_sem.at[9])
    loads[0].start()
    loads[1].start()

    @pl.when(stage == 3)
    def _():
        load_loss.start()
    for copy in loads[2:]:
        copy.start()
    start_loads(stage, nb_hbm, nbuf, nb_sem)

    barrier = pltpu.get_barrier_semaphore()

    def greet(d, _):
        other = lax.rem(me + d, 16)
        pl.semaphore_signal(barrier, inc=1, device_id={"data": lax.div(other, 4), "stage": lax.rem(other, 4)}, device_id_type=MESH)
        return 0
    lax.fori_loop(1, 16, greet, 0)

    loads[0].wait()
    loads[1].wait()
    up_bf[...] = up32[...].astype(BF16)
    loads[2].wait()
    down_bf[...] = down32[...].astype(BF16)
    pl.semaphore_wait(barrier, 15)

    @pl.when(stage == 3)
    def _():
        load_loss.wait()

    def chunk_rows(k):
        return pl.ds(pl.multiple_of(k * chunk, chunk), chunk)

    def pass_down(k):
        rows = chunk_rows(k)
        return pltpu.make_async_remote_copy(src_ref=dxbuf.at[rows], dst_ref=gbuf.at[rows], send_sem=g_send.at[k], recv_sem=g_recv.at[k],
                                            device_id={"stage": jnp.maximum(stage - 1, 0)}, device_id_type=MESH)

    def prepare(k):
        rows = chunk_rows(k)
        pre = jnp.dot(acts[rows, :], up_bf[...], preferred_element_type=F32)
        sq = pre * pre
        half_t = 0.5 * jnp.tanh(pre * (SQRT_TWO_PI + (SQRT_TWO_PI * GELU_CUBIC) * sq))
        prob = 0.5 + half_t
        rest = 0.5 - half_t
        hid[rows, :] = (pre * prob).astype(BF16)
        slope[rows, :] = prob + (prob * rest) * pre * (2.0 * SQRT_TWO_PI + (6.0 * SQRT_TWO_PI * GELU_CUBIC) * sq)

    def backward(k):
        rows = chunk_rows(k)

        @pl.when(stage < 3)
        def _():
            pass_down(k).wait_recv()
        grad = gbuf[rows, :]
        d_pre = (mat_nt(grad, down_bf[...]) * slope[rows, :]).astype(BF16)
        dpre[rows, :] = d_pre

        @pl.when(stage > 0)
        def _():
            dxbuf[rows, :] = (grad.astype(F32) + mat_nt(d_pre, up_bf[...])).astype(BF16)
            pass_down(k).start()

    def tick(t, _):
        upper = jnp.where(stage >= 2, 1, 0)
        is_prep = upper * (1 - lax.rem(t, 2)) + (1 - upper) * (1 - lax.div(t, N_CHUNK))
        k = upper * lax.div(t, 2) + (1 - upper) * lax.rem(t, N_CHUNK)

        @pl.when(is_prep == 1)
        def _():
            prepare(k)

        @pl.when(is_prep == 0)
        def _():
            backward(k)
        return 0
    lax.fori_loop(0, 2 * N_CHUNK, tick, 0)

    def rs_copy(src, dst, sem, peer):
        return pltpu.make_async_remote_copy(src_ref=src, dst_ref=dst, send_sem=rs_send.at[sem], recv_sem=rs_recv.at[sem], device_id={"data": peer}, device_id_type=MESH)

    def v_first(sub, c):
        yy = (1 - y) if sub == 0 else y
        return rs_copy(gv.at[down_rows(1 - z, yy, 128 * c, 128)], rv1.at[sub, pl.ds(128 * c, 128)], 2 * sub + c, z_peer)

    def u_first(sub, c):
        zz = (1 - z) if sub == 0 else z
        return rs_copy(gu.at[up_rows(zz, 1 - y, 32 * c, 32)], ru1.at[sub, pl.ds(32 * c, 32)], 4 + 2 * sub + c, y_peer)

    def v_second(c):
        return rs_copy(gv.at[down_rows(z, 1 - y, 128 * c, 128)], rv2.at[pl.ds(128 * c, 128)], 8 + c, y_peer)

    def u_second(c):
        return rs_copy(gu.at[up_rows(1 - z, y, 32 * c, 32)], ru2.at[pl.ds(32 * c, 32)], 10 + c, z_peer)

    loads[3].wait()
    gv[...] += mat_tn(hid[...], gbuf[...])
    for sub in range(2):
        for c in range(2):
            v_first(sub, c).start()
    loads[4].wait()
    gu[...] += mat_tn(acts[...], dpre[...])
    for sub in range(2):
        for c in range(2):
            u_first(sub, c).start()
    for c in range(2):
        v_first(0, c).wait_recv()
        rows = down_rows(z, 1 - y, 128 * c, 128)
        gv[rows, :] += rv1[0, 128 * c:128 * (c + 1), :]
        v_second(c).start()
        u_first(0, c).wait_recv()
        rows = up_rows(1 - z, y, 32 * c, 32)
        gu[rows, :] += ru1[0, 32 * c:32 * (c + 1), :]
        u_second(c).start()
    acc = jnp.zeros((8, 128), F32)

    def fold(tile, acc):
        sq = tile * tile
        sq = jnp.sum(sq.reshape(sq.shape[0] // 8, 8, sq.shape[1]), axis=0)
        for i in range(0, sq.shape[1], 128):
            acc = acc + sq[:, i:i + 128]
        return acc

    for c in range(2):
        v_first(1, c).wait_recv()
        v_second(c).wait_recv()
        rows = down_rows(z, y, 128 * c, 128)
        mean = (gv[rows, :] + rv1[1, 128 * c:128 * (c + 1), :] + rv2[128 * c:128 * (c + 1), :]) * 0.25
        mean_down[rows, :] = mean
        acc = fold(mean, acc)
        u_first(1, c).wait_recv()
        u_second(c).wait_recv()
        rows = up_rows(z, y, 32 * c, 32)
        mean = (gu[rows, :] + ru1[1, 32 * c:32 * (c + 1), :] + ru2[32 * c:32 * (c + 1), :]) * 0.25
        mean_up[rows, :] = mean
        acc = fold(mean, acc)

    def sq_copy(other, slot):
        return pltpu.make_async_remote_copy(src_ref=sq_all.at[slot], dst_ref=sq_all.at[slot], send_sem=sq_send.at[other], recv_sem=sq_recv.at[slot],
                                            device_id={"data": lax.div(other, 4), "stage": lax.rem(other, 4)}, device_id_type=MESH)

    sq_all[me] = acc

    def tell(d, _):
        sq_copy(lax.rem(me + d, 16), me).start()
        return 0
    lax.fori_loop(1, 16, tell, 0)
    for copy in loads[5:]:
        copy.wait()

    def hear(d, _):
        other = lax.rem(me + d, 16)
        sq_copy(other, other).wait_recv()
        return 0
    lax.fori_loop(1, 16, hear, 0)
    total = sq_all[0]
    for i in range(1, 16):
        total = total + sq_all[i]
    total = jnp.sum(jnp.sum(total, axis=0, keepdims=True), axis=1, keepdims=True)
    clip = jnp.minimum(1.0, norm_ref[0] / (jnp.sqrt(total) + NORM_EPS))
    clip_out[...] = jnp.broadcast_to(clip, clip_out.shape)

    rate = rate_ref[0]
    new_up, _, _ = adamw_update(up32[own_up, :], mq_up[0], mq_up[1], mean_up[own_up, :], clip, rate)
    up_own[own_up, :] = new_up.astype(BF16) * jnp.asarray(0.5, BF16)
    new_down, _, _ = adamw_update(down32[own_down, :], mq_down[0], mq_down[1], mean_down[own_down, :], clip, rate)
    down_own[own_down, :] = new_down.astype(BF16)

    def gather(which, up, down):
        def copy(ref, rows, sem, peer):
            return pltpu.make_async_remote_copy(src_ref=ref.at[rows], dst_ref=ref.at[rows], send_sem=ag_send.at[which * 6 + sem], recv_sem=ag_recv.at[which * 6 + sem],
                                                device_id={"data": peer}, device_id_type=MESH)

        sends = [copy(up, own_up, 0, z_peer), copy(down, own_down, 3, y_peer), copy(up, own_up, 1, y_peer), copy(down, own_down, 4, z_peer)]
        relays = [copy(up, up_rows(1 - z, y), 2, y_peer), copy(down, down_rows(z, 1 - y), 5, z_peer)]
        arrive_first = [copy(up, up_rows(1 - z, y), 0, z_peer), copy(down, down_rows(z, 1 - y), 3, y_peer)]
        arrive_rest = [copy(up, up_rows(z, 1 - y), 1, y_peer), copy(down, down_rows(1 - z, y), 4, z_peer),
                       copy(up, up_rows(1 - z, 1 - y), 2, y_peer), copy(down, down_rows(1 - z, 1 - y), 5, z_peer)]

        def begin():
            for c in sends:
                c.start()

        def relay():
            for a, c in zip(arrive_first, relays):
                a.wait_recv()
                c.start()

        def finish():
            for c in arrive_rest:
                c.wait_recv()

        def drain():
            for c in sends + relays:
                c.wait_send()
        return begin, relay, finish, drain

    own_begin, own_relay, own_finish, own_drain = gather(0, up_own, down_own)
    aux_begin, aux_relay, aux_finish, aux_drain = gather(1, up_aux, down_aux)
    mean_begin, mean_relay, mean_finish, mean_drain = gather(2, mean_up, mean_down)

    def feed():
        peer = 3 - stage
        return [pltpu.make_async_remote_copy(src_ref=own.at[rows], dst_ref=aux.at[rows], send_sem=aux_send.at[i], recv_sem=aux_recv.at[i], device_id={"stage": peer}, device_id_type=MESH)
                for i, (own, aux, rows) in enumerate([(up_own, up_aux, own_up), (down_own, down_aux, own_down)])]

    @pl.when(stage < 2)
    def _():
        for c in feed():
            c.start()
    own_begin()
    own_relay()

    @pl.when(stage >= 2)
    def _():
        for c in feed():
            c.wait_recv()
        aux_begin()
        aux_relay()
    mean_begin()

    def relay_mean(now):
        @pl.when(now)
        def _():
            mean_relay()

    forward_part(stage, own_finish, aux_finish, relay_mean, nb_hbm, up_own, down_own, up_aux, down_aux, out_hbm, nbuf, xin, yout, nb_sem, out_sem, send_sem, recv_sem)

    mean_finish()
    store_up = pltpu.make_async_copy(mean_up, mean_up_hbm, in_sem.at[0])
    store_down = pltpu.make_async_copy(mean_down, mean_down_hbm, in_sem.at[1])
    store_up.start()
    store_down.start()

    @pl.when(stage > 0)
    def _():
        for k in range(N_CHUNK):
            pass_down(k).wait_send()
    for c in range(2):
        for sub in range(2):
            v_first(sub, c).wait_send()
            u_first(sub, c).wait_send()
        v_second(c).wait_send()
        u_second(c).wait_send()

    def told(d, _):
        sq_copy(lax.rem(me + d, 16), me).wait_send()
        return 0
    lax.fori_loop(1, 16, told, 0)
    own_drain()
    mean_drain()

    @pl.when(stage < 2)
    def _():
        for c in feed():
            c.wait_send()

    @pl.when(stage >= 2)
    def _():
        aux_drain()
    store_up.wait()
    store_down.wait()


def fused_step(master_up, master_down, m1_up, m1_down, m2_up, m2_down, grad_up, grad_down, acts, loss_grad, next_batch, learn_rate, max_norm):
    n_micro = next_batch.shape[0]
    n_tok, width = acts.shape
    hidden = master_up.shape[1]
    hbm = pl.BlockSpec(memory_space=pl.ANY)
    smem = pl.BlockSpec(memory_space=pltpu.SMEM)
    vmem = pltpu.VMEM
    dma = pltpu.SemaphoreType.DMA
    return pl.pallas_call(
        step_kernel,
        name="pipeline_step",
        out_shape=[jax.ShapeDtypeStruct(next_batch.shape, BF16), jax.ShapeDtypeStruct((width, hidden), F32), jax.ShapeDtypeStruct((hidden, width), F32), jax.ShapeDtypeStruct((8, 128), F32)],
        in_specs=[hbm] * 11 + [smem] * 2,
        out_specs=[hbm, hbm, hbm, pl.BlockSpec(memory_space=pltpu.VMEM)],
        scratch_shapes=[
            vmem((width, hidden), F32), vmem((hidden, width), F32),
            vmem((width, hidden), F32), vmem((hidden, width), F32),
            vmem((width, hidden), F32), vmem((hidden, width), F32),
            vmem((n_tok, width), BF16), vmem((n_tok, width), BF16), vmem((n_tok, width), BF16),
            vmem((n_tok, hidden), BF16), vmem((n_tok, hidden), F32), vmem((n_tok, hidden), BF16),
            vmem((width, hidden), BF16), vmem((hidden, width), BF16),
            vmem((2, width // 4, hidden), F32), vmem((2, hidden // 4, width), F32),
            vmem((width // 4, hidden), F32), vmem((hidden // 4, width), F32),
            vmem((2, width // 4, hidden), F32), vmem((2, hidden // 4, width), F32),
            vmem((width, hidden), BF16), vmem((hidden, width), BF16),
            vmem((width, hidden), BF16), vmem((hidden, width), BF16),
            vmem((16, 8, 128), F32),
            vmem(next_batch.shape, BF16), vmem(next_batch.shape, BF16), vmem(next_batch.shape, BF16),
            dma((10,)), dma((N_CHUNK,)), dma((N_CHUNK,)), dma((12,)), dma((12,)), dma((16,)), dma((16,)), dma((18,)), dma((18,)), dma((2,)), dma((2,)),
            dma((n_micro,)), dma((n_micro,)), dma((n_micro,)), dma((n_micro,)),
        ],
        compiler_params=pltpu.CompilerParams(collective_id=1, has_side_effects=True, vmem_limit_bytes=63 * 1024 * 1024),
    )(master_up, master_down, m1_up, m1_down, m2_up, m2_down, grad_up, grad_down, acts, loss_grad, next_batch, learn_rate, max_norm)


def solution(mesh):
    def local_step(master_up, master_down, mom1_up, mom1_down, mom2_up, mom2_down, grad_up, grad_down, stage_acts, loss_grad, next_batch, learn_rate, max_norm):
        stage_outs, gbar_up, gbar_down, clip = fused_step(
            master_up[0], master_down[0], mom1_up[0], mom1_down[0], mom2_up[0], mom2_down[0], grad_up[0, 0], grad_down[0, 0],
            stage_acts[0], loss_grad, next_batch, learn_rate.reshape(1), max_norm.reshape(1))
        clip_scale = clip[0, 0]
        new_up, new_m1_up, new_m2_up = adamw_update(master_up[0], mom1_up[0], mom2_up[0], gbar_up, clip_scale, learn_rate)
        new_down, new_m1_down, new_m2_down = adamw_update(master_down[0], mom1_down[0], mom2_down[0], gbar_down, clip_scale, learn_rate)
        return (new_up[None], new_down[None], new_m1_up[None], new_m1_down[None], new_m2_up[None], new_m2_down[None], stage_outs[None])

    w_spec = P('stage', None, None)
    g_spec = P('data', 'stage', None, None)
    in_specs = (w_spec, w_spec, w_spec, w_spec, w_spec, w_spec, g_spec, g_spec, P('stage', 'data', None), P('data', None), P(None, 'data', None), P(), P())
    out_specs = (w_spec, w_spec, w_spec, w_spec, w_spec, w_spec, P('stage', None, 'data', None))
    return jax.shard_map(local_step, mesh=mesh, in_specs=in_specs, out_specs=out_specs, check_vma=False)
```

time: 247 us -> 128 us (0.52)
  waiting for transfers between devices: 94.4 us -> 0 us
  Pallas kernels: 49.4 us -> 107 us
  matrix products: 33.8 us -> 0 us
  starting transfers between devices: 22.2 us -> 0 us
  between operations: 17.7 us -> 1.94 us
  blocking collectives: 6.46 us -> 0 us
  other arithmetic: 14.2 us -> 10.6 us
    psum x1 -> x0, waiting for transfers between devices: 69.7 us -> none  [local_step(): gbar_up = lax.psum(grad_up[0, 0] + mat_tn(stage_in, d_pre), 'data') / n_reps]
    pallas_call x1, Pallas kernels: 49.4 us -> 107 us  [fused_step(): pl.pallas_call(step_kernel, name='pipeline_step', out_shape=[jax.ShapeDty...]
    dot_general x6 -> x0, matrix products: 33.8 us -> none  [the longest x3 18.3 us: mat_nt(): lax.dot_general(left, right, (((1,), (1,)), ((), ())), preferred_element_...]
    ppermute x5 -> x0, waiting for transfers between devices: 24.7 us -> none  [the longest x1 11.2 us: local_step(): up_aux = lax.ppermute(up_half, 'stage', [(0, 3), (1, 2)])]
    ppermute x5 -> x0, starting transfers between devices: 22.2 us -> none  [the longest x3 19.6 us: local_step(): received = lax.ppermute(d_rows, 'stage', down_pairs)]
    psum x1 -> x0, blocking collectives: 6.46 us -> none  [local_step(): grad_norm = jnp.sqrt(lax.psum(local_sq, 'stage'))]
    convert_element_type x2 -> x0, other arithmetic: 5.6 us -> none  [the longest x1 4.19 us: local_step(): down_new = new_down.astype(BF16)]
    broadcast_in_dim x0 -> x1, other arithmetic: none -> 5.27 us  [local_step(): new_m2_down[None]]
  transfers between devices with their start and end apart: 6 -> 0, of which waited for: 6 -> 0; matrix products, arithmetic and copies ran while one was open for 1% -> 0% of each run, Pallas kernels for 0% -> 0%
where the time goes in v2:
time: 128 us
  Pallas kernels  107 us (84%)
  other arithmetic  10.6 us (8%)
  local copies, waits for them, and re-layouts  8.73 us (7%)
  between operations  1.94 us (2%)
    pallas_call x1, Pallas kernels, fused_step(): pl.pallas_call(step_kernel, name='pipeline_step', out_shape=[jax.ShapeDty...  107 us
    unnamed x1, local copies, waits for them, and re-layouts  7.52 us
    broadcast_in_dim x1, other arithmetic, local_step(): new_m2_up[None]  5.35 us
    broadcast_in_dim x1, other arithmetic, local_step(): new_m2_down[None]  5.27 us

profile of v2, /device:TPU:3, one launch (start us, length us, event | category | flops | bytes accessed | tf_op | source)
XLA Modules:
  0.0 128.1 jit_solution(5317113620207091485)
XLA Ops:
  1.9 106.9 %pipeline_step.1 = (bf16[16,1024,256]{2,1,0:T(8,128)(2,1)}, f32[256,1024]{1,0:T(8,128)}, f32[1024,256]{1,0:T(8,128)}, f32[8,128]{1,0:T(8,128)}) custom-call(f32[256,1024]{1,0:T(8,128)} %bitcast.41, f32[1024,256]{1,0:T(8,128)} %bitcast.38, f32[256,1024]{1,0:T(8,128)} %bitcast.42, f32[1024,256]{1,0:T(8,128)} %bitcast.39, f32[256,1024]{1,0:T(8,128)} %bitcast.43, ...), custom_call_target="tpu_custom_call" | custom-call | tf_op jit(solution)/shard_map/pipeline_step/pallas_call | solution.py:495
  108.8 1.2 slice.3
  110.0 5.3 %fusion.4 = (f32[1,1024,256]{2,1,0:T(8,128)}, f32[1,1024,256]{2,1,0:T(8,128)}, f32[1,1024,256]{2,1,0:T(8,128)}) fusion(f32[1024,256]{1,0:T(8,128)} %get-tuple-element.13, f32[]{:T(128)} %bitcast.11, f32[1,1024,256]{2,1,0:T(8,128)} %param.18, f32[1,1024,256]{2,1,0:T(8,128)} %param.16, f32[]{:T(128)} %copy.21, f32[1,1024,256]{2,1,0:T(8,128)} %param.14), kind=kLoop, calls=%fused_computation.10 | loop fusion | flops 4194304 | bytes 7340040 | tf_op jit(solution)/shard_map/broadcast_in_dim | solution.py:530
  115.3 5.3 %fusion.5 = (f32[1,256,1024]{2,1,0:T(8,128)}, f32[1,256,1024]{2,1,0:T(8,128)}, f32[1,256,1024]{2,1,0:T(8,128)}) fusion(f32[256,1024]{1,0:T(8,128)} %get-tuple-element.12, f32[]{:T(128)} %bitcast.11, f32[1,256,1024]{2,1,0:T(8,128)} %param.17, f32[1,256,1024]{2,1,0:T(8,128)} %param.15, f32[]{:T(128)} %copy.21, f32[1,256,1024]{2,1,0:T(8,128)} %param.13), kind=kLoop, calls=%fused_computation.11 | loop fusion | flops 4194304 | bytes 7340040 | tf_op jit(solution)/shard_map/broadcast_in_dim | solution.py:530
  120.6 7.5 %copy.23 = bf16[1,16,1024,256]{3,2,1,0:T(8,128)(2,1)} copy(bf16[1,16,1024,256]{3,2,1,0:T(8,128)(2,1)} %bitcast.37) | data formatting | bytes 16777216

commit v3 on v2

--- a/solution.py
+++ b/solution.py
@@ -16,6 +16,8 @@
 
 N_SENT = 6
 N_CHUNK = 4
+N_LATE = 5
+N_TWICE = 2
 MESH = pl.DeviceIdType.MESH
 BF16 = jnp.bfloat16
 F32 = jnp.float32
@@ -33,8 +35,8 @@
     scaled = clip_scale * grad_avg
     new_first = BETA1 * first_mom + (1.0 - BETA1) * scaled
     new_second = BETA2 * second_mom + (1.0 - BETA2) * scaled * scaled
-    first_hat = new_first / (1.0 - BETA1 ** ADAM_STEP)
-    second_hat = new_second / (1.0 - BETA2 ** ADAM_STEP)
+    first_hat = new_first * (1.0 / (1.0 - BETA1 ** ADAM_STEP))
+    second_hat = new_second * (1.0 / (1.0 - BETA2 ** ADAM_STEP))
     new_master = master - learn_rate * (first_hat / (jnp.sqrt(second_hat) + ADAM_EPS) + WEIGHT_DECAY * master)
     return new_master, new_first, new_second
 
@@ -52,7 +54,13 @@
     dst[...] = (x.astype(F32) + y).astype(BF16)
 
 
-def forward_part(stage, own_ready, aux_ready, relay_mean, nb_hbm, up_own, down_own, up_aux, down_aux, out_hbm, nbuf, xin, yout, nb_sem, out_sem, send_sem, recv_sem):
+def mixed(k, n_micro):
+    before = lax.div(k * N_SENT, n_micro)
+    is_sent = lax.div((k + 1) * N_SENT, n_micro) - before
+    return is_sent, is_sent * (n_micro - N_SENT + before) + (1 - is_sent) * (k - before)
+
+
+def forward_part(stage, own_ready, aux_ready, relay_mean, nb_hbm, up_own, down_own, up_aux, down_aux, up_two, down_two, out_hbm, late_hbm, nbuf, xin, yout, nb_sem, out_sem, send_sem, recv_sem, two_send, two_recv):
     n_micro = nbuf.shape[0]
     n_kept = n_micro - N_SENT
 
@@ -70,17 +78,16 @@
 
     def rotated(j):
         return lax.rem(j + n_kept, n_micro)
-
-    def mixed(k):
-        before = lax.div(k * N_SENT, n_micro)
-        is_sent = lax.div((k + 1) * N_SENT, n_micro) - before
-        return is_sent, is_sent * (n_kept + before) + (1 - is_sent) * (k - before)
 
     def finish_stores():
         def body(i, _):
             store(i).wait()
             return 0
         lax.fori_loop(0, n_micro, body, 0)
+
+    def hand_over():
+        return [pltpu.make_async_remote_copy(src_ref=aux, dst_ref=two, send_sem=two_send.at[i], recv_sem=two_recv.at[i], device_id={"stage": 3}, device_id_type=MESH)
+                for i, (aux, two) in enumerate([(up_aux, up_two), (down_aux, down_two)])]
 
     def finish_sends(first, count):
         def body(i, _):
@@ -126,23 +133,25 @@
     @pl.when(stage == 2)
     def _():
         aux_ready()
-        own_ready()
+        for copy in hand_over():
+            copy.start()
 
         def body(k, _):
-            is_sent, i = mixed(k)
+            _, i = mixed(k, n_micro)
             arrived(i)
 
-            @pl.when(is_sent == 0)
+            @pl.when(i < n_kept - N_TWICE)
             def _():
                 stage_rows(xin.at[i], up_aux, down_aux, xin.at[i])
             stage_rows(xin.at[i], up_own, down_own, yout.at[i])
             push(yout, i, 3).start()
             store(i).start()
-            relay_mean(k == 6)
             return 0
         lax.fori_loop(0, n_micro, body, 0)
         finish_sends(0, n_micro)
         finish_stores()
+        for copy in hand_over():
+            copy.wait_send()
 
     @pl.when(stage == 3)
     def _():
@@ -151,21 +160,49 @@
         def first(j, _):
             load(j).wait()
             stage_rows(nbuf.at[j], up_aux, down_aux, nbuf.at[j])
+
+            @pl.when(j == n_kept - N_TWICE)
+            def _():
+                for copy in hand_over():
+                    copy.wait_recv()
+
+            @pl.when(j >= n_kept - N_TWICE)
+            def _():
+                stage_rows(nbuf.at[j], up_two, down_two, nbuf.at[j])
             push(nbuf, j, 2).start()
             return 0
         lax.fori_loop(0, n_kept, first, 0)
-        own_ready()
 
         def body(k, _):
-            _, i = mixed(k)
+            _, i = mixed(k, n_micro)
             arrived(i)
             stage_rows(xin.at[i], up_own, down_own, yout.at[i])
             store(i).start()
-            relay_mean(k == 1)
-            return 0
-        lax.fori_loop(0, n_micro, body, 0)
+            return 0
+        lax.fori_loop(0, n_micro - N_LATE, body, 0)
+
+        def late(k):
+            _, i = mixed(k, n_micro)
+            return i, pltpu.make_async_copy(xin.at[i], late_hbm.at[k - (n_micro - N_LATE)], out_sem.at[i])
+
+        def save(k, _):
+            i, copy = late(k)
+            arrived(i)
+            copy.start()
+            return 0
+        lax.fori_loop(n_micro - N_LATE, n_micro, save, 0)
+
+        def stored(k, _):
+            _, i = mixed(k, n_micro)
+            store(i).wait()
+            return 0
+        lax.fori_loop(0, n_micro - N_LATE, stored, 0)
+
+        def saved(k, _):
+            late(k)[1].wait()
+            return 0
+        lax.fori_loop(n_micro - N_LATE, n_micro, saved, 0)
         finish_sends(0, n_kept)
-        finish_stores()
 
 
 def start_loads(stage, nb_hbm, nbuf, nb_sem):
@@ -187,11 +224,11 @@
 
 
 def step_kernel(up_hbm, down_hbm, m1_up_hbm, m1_down_hbm, m2_up_hbm, m2_down_hbm, gu_hbm, gv_hbm, acts_hbm, loss_hbm, nb_hbm, rate_ref, norm_ref,
-                out_hbm, mean_up_hbm, mean_down_hbm, clip_out,
+                out_hbm, mean_up_hbm, mean_down_hbm, clip_out, late_hbm, w_up_hbm, w_down_hbm,
                 up32, down32, gu, gv, mean_up, mean_down, acts, gbuf, dxbuf, hid, slope, dpre, up_bf, down_bf,
-                ru1, rv1, ru2, rv2, mq_up, mq_down, up_own, down_own, up_aux, down_aux, sq_all, nbuf, xin, yout,
+                ru1, rv1, ru2, rv2, m_up, m_down, up_own, down_own, up_aux, down_aux, up_two, down_two, sq_all, nbuf, xin, yout,
                 in_sem, g_send, g_recv, rs_send, rs_recv, sq_send, sq_recv, ag_send, ag_recv, aux_send, aux_recv,
-                nb_sem, out_sem, send_sem, recv_sem):
+                nb_sem, out_sem, send_sem, recv_sem, two_send, two_recv):
     stage = lax.axis_index("stage")
     data = lax.axis_index("data")
     z = lax.div(data, 2)
@@ -215,10 +252,10 @@
         pltpu.make_async_copy(down_hbm, down32, in_sem.at[2]),
         pltpu.make_async_copy(gv_hbm, gv, in_sem.at[3]),
         pltpu.make_async_copy(gu_hbm, gu, in_sem.at[4]),
-        pltpu.make_async_copy(m1_up_hbm.at[own_up], mq_up.at[0], in_sem.at[5]),
-        pltpu.make_async_copy(m2_up_hbm.at[own_up], mq_up.at[1], in_sem.at[6]),
-        pltpu.make_async_copy(m1_down_hbm.at[own_down], mq_down.at[0], in_sem.at[7]),
-        pltpu.make_async_copy(m2_down_hbm.at[own_down], mq_down.at[1], in_sem.at[8]),
+        pltpu.make_async_copy(m1_up_hbm, m_up.at[0], in_sem.at[5]),
+        pltpu.make_async_copy(m2_up_hbm, m_up.at[1], in_sem.at[6]),
+        pltpu.make_async_copy(m1_down_hbm, m_down.at[0], in_sem.at[7]),
+        pltpu.make_async_copy(m2_down_hbm, m_down.at[1], in_sem.at[8]),
     ]
     load_loss = pltpu.make_async_copy(loss_hbm, gbuf, in_sem.at[9])
     loads[0].start()
@@ -357,6 +394,39 @@
         mean_up[rows, :] = mean
         acc = fold(mean, acc)
 
+    def gather(which, up, down):
+        def copy(ref, rows, sem, peer):
+            return pltpu.make_async_remote_copy(src_ref=ref.at[rows], dst_ref=ref.at[rows], send_sem=ag_send.at[which * 6 + sem], recv_sem=ag_recv.at[which * 6 + sem],
+                                                device_id={"data": peer}, device_id_type=MESH)
+
+        sends = [copy(up, own_up, 0, z_peer), copy(down, own_down, 3, y_peer), copy(up, own_up, 1, y_peer), copy(down, own_down, 4, z_peer)]
+        relays = [copy(up, up_rows(1 - z, y), 2, y_peer), copy(down, down_rows(z, 1 - y), 5, z_peer)]
+        arrive_first = [copy(up, up_rows(1 - z, y), 0, z_peer), copy(down, down_rows(z, 1 - y), 3, y_peer)]
+        arrive_rest = [copy(up, up_rows(z, 1 - y), 1, y_peer), copy(down, down_rows(1 - z, y), 4, z_peer),
+                       copy(up, up_rows(1 - z, 1 - y), 2, y_peer), copy(down, down_rows(1 - z, 1 - y), 5, z_peer)]
+
+        def begin():
+            for c in sends:
+                c.start()
+
+        def relay():
+            for a, c in zip(arrive_first, relays):
+                a.wait_recv()
+                c.start()
+
+        def finish():
+            for c in arrive_rest:
+                c.wait_recv()
+
+        def drain():
+            for c in sends + relays:
+                c.wait_send()
+        return begin, relay, finish, drain
+
+    own_begin, own_relay, own_finish, own_drain = gather(0, up_own, down_own)
+    aux_begin, aux_relay, aux_finish, aux_drain = gather(1, up_aux, down_aux)
+    mean_begin, mean_relay, mean_finish, mean_drain = gather(2, mean_up, mean_down)
+
     def sq_copy(other, slot):
         return pltpu.make_async_remote_copy(src_ref=sq_all.at[slot], dst_ref=sq_all.at[slot], send_sem=sq_send.at[other], recv_sem=sq_recv.at[slot],
                                             device_id={"data": lax.div(other, 4), "stage": lax.rem(other, 4)}, device_id_type=MESH)
@@ -369,6 +439,12 @@
     lax.fori_loop(1, 16, tell, 0)
     for copy in loads[5:]:
         copy.wait()
+
+    @pl.when(stage >= 2)
+    def _():
+        mean_begin()
+        mean_relay()
+        mean_finish()
 
     def hear(d, _):
         other = lax.rem(me + d, 16)
@@ -383,43 +459,17 @@
     clip_out[...] = jnp.broadcast_to(clip, clip_out.shape)
 
     rate = rate_ref[0]
-    new_up, _, _ = adamw_update(up32[own_up, :], mq_up[0], mq_up[1], mean_up[own_up, :], clip, rate)
-    up_own[own_up, :] = new_up.astype(BF16) * jnp.asarray(0.5, BF16)
-    new_down, _, _ = adamw_update(down32[own_down, :], mq_down[0], mq_down[1], mean_down[own_down, :], clip, rate)
-    down_own[own_down, :] = new_down.astype(BF16)
-
-    def gather(which, up, down):
-        def copy(ref, rows, sem, peer):
-            return pltpu.make_async_remote_copy(src_ref=ref.at[rows], dst_ref=ref.at[rows], send_sem=ag_send.at[which * 6 + sem], recv_sem=ag_recv.at[which * 6 + sem],
-                                                device_id={"data": peer}, device_id_type=MESH)
-
-        sends = [copy(up, own_up, 0, z_peer), copy(down, own_down, 3, y_peer), copy(up, own_up, 1, y_peer), copy(down, own_down, 4, z_peer)]
-        relays = [copy(up, up_rows(1 - z, y), 2, y_peer), copy(down, down_rows(z, 1 - y), 5, z_peer)]
-        arrive_first = [copy(up, up_rows(1 - z, y), 0, z_peer), copy(down, down_rows(z, 1 - y), 3, y_peer)]
-        arrive_rest = [copy(up, up_rows(z, 1 - y), 1, y_peer), copy(down, down_rows(1 - z, y), 4, z_peer),
-                       copy(up, up_rows(1 - z, 1 - y), 2, y_peer), copy(down, down_rows(1 - z, 1 - y), 5, z_peer)]
-
-        def begin():
-            for c in sends:
-                c.start()
-
-        def relay():
-            for a, c in zip(arrive_first, relays):
-                a.wait_recv()
-                c.start()
-
-        def finish():
-            for c in arrive_rest:
-                c.wait_recv()
-
-        def drain():
-            for c in sends + relays:
-                c.wait_send()
-        return begin, relay, finish, drain
-
-    own_begin, own_relay, own_finish, own_drain = gather(0, up_own, down_own)
-    aux_begin, aux_relay, aux_finish, aux_drain = gather(1, up_aux, down_aux)
-    mean_begin, mean_relay, mean_finish, mean_drain = gather(2, mean_up, mean_down)
+    whole = jnp.where(stage >= 2, 1, 0)
+
+    def renew(t, _):
+        rows = pl.ds(pl.multiple_of(64 * (whole * t + (1 - whole) * (2 * y + z)), 64), 64)
+        new_up, _, _ = adamw_update(up32[rows, :], m_up[0, rows, :], m_up[1, rows, :], mean_up[rows, :], clip, rate)
+        up_own[rows, :] = new_up.astype(BF16) * jnp.asarray(0.5, BF16)
+        rows = pl.ds(pl.multiple_of(256 * (whole * t + (1 - whole) * (2 * z + y)), 256), 256)
+        new_down, _, _ = adamw_update(down32[rows, :], m_down[0, rows, :], m_down[1, rows, :], mean_down[rows, :], clip, rate)
+        down_own[rows, :] = new_down.astype(BF16)
+        return 0
+    lax.fori_loop(0, 1 + 3 * whole, renew, 0)
 
     def feed():
         peer = 3 - stage
@@ -430,8 +480,9 @@
     def _():
         for c in feed():
             c.start()
-    own_begin()
-    own_relay()
+        own_begin()
+        own_relay()
+        mean_begin()
 
     @pl.when(stage >= 2)
     def _():
@@ -439,20 +490,25 @@
             c.wait_recv()
         aux_begin()
         aux_relay()
-    mean_begin()
 
     def relay_mean(now):
         @pl.when(now)
         def _():
             mean_relay()
 
-    forward_part(stage, own_finish, aux_finish, relay_mean, nb_hbm, up_own, down_own, up_aux, down_aux, out_hbm, nbuf, xin, yout, nb_sem, out_sem, send_sem, recv_sem)
-
-    mean_finish()
+    forward_part(stage, own_finish, aux_finish, relay_mean, nb_hbm, up_own, down_own, up_aux, down_aux, up_two, down_two, out_hbm, late_hbm, nbuf, xin, yout, nb_sem, out_sem, send_sem, recv_sem, two_send, two_recv)
+
+    @pl.when(stage < 2)
+    def _():
+        mean_finish()
     store_up = pltpu.make_async_copy(mean_up, mean_up_hbm, in_sem.at[0])
     store_down = pltpu.make_async_copy(mean_down, mean_down_hbm, in_sem.at[1])
+    store_w_up = pltpu.make_async_copy(up_own, w_up_hbm, in_sem.at[2])
+    store_w_down = pltpu.make_async_copy(down_own, w_down_hbm, in_sem.at[3])
     store_up.start()
     store_down.start()
+    store_w_up.start()
+    store_w_down.start()
 
     @pl.when(stage > 0)
     def _():
@@ -469,11 +525,11 @@
         sq_copy(lax.rem(me + d, 16), me).wait_send()
         return 0
     lax.fori_loop(1, 16, told, 0)
-    own_drain()
     mean_drain()
 
     @pl.when(stage < 2)
     def _():
+        own_drain()
         for c in feed():
             c.wait_send()
 
@@ -482,6 +538,8 @@
         aux_drain()
     store_up.wait()
     store_down.wait()
+    store_w_up.wait()
+    store_w_down.wait()
 
 
 def fused_step(master_up, master_down, m1_up, m1_down, m2_up, m2_down, grad_up, grad_down, acts, loss_grad, next_batch, learn_rate, max_norm):
@@ -495,9 +553,10 @@
     return pl.pallas_call(
         step_kernel,
         name="pipeline_step",
-        out_shape=[jax.ShapeDtypeStruct(next_batch.shape, BF16), jax.ShapeDtypeStruct((width, hidden), F32), jax.ShapeDtypeStruct((hidden, width), F32), jax.ShapeDtypeStruct((8, 128), F32)],
+        out_shape=[jax.ShapeDtypeStruct(next_batch.shape, BF16), jax.ShapeDtypeStruct((width, hidden), F32), jax.ShapeDtypeStruct((hidden, width), F32), jax.ShapeDtypeStruct((8, 128), F32),
+                   jax.ShapeDtypeStruct((N_LATE,) + next_batch.shape[1:], BF16), jax.ShapeDtypeStruct((width, hidden), BF16), jax.ShapeDtypeStruct((hidden, width), BF16)],
         in_specs=[hbm] * 11 + [smem] * 2,
-        out_specs=[hbm, hbm, hbm, pl.BlockSpec(memory_space=pltpu.VMEM)],
+        out_specs=[hbm, hbm, hbm, pl.BlockSpec(memory_space=pltpu.VMEM), hbm, hbm, hbm],
         scratch_shapes=[
             vmem((width, hidden), F32), vmem((hidden, width), F32),
             vmem((width, hidden), F32), vmem((hidden, width), F32),
@@ -507,26 +566,150 @@
             vmem((width, hidden), BF16), vmem((hidden, width), BF16),
             vmem((2, width // 4, hidden), F32), vmem((2, hidden // 4, width), F32),
             vmem((width // 4, hidden), F32), vmem((hidden // 4, width), F32),
-            vmem((2, width // 4, hidden), F32), vmem((2, hidden // 4, width), F32),
+            vmem((2, width, hidden), F32), vmem((2, hidden, width), F32),
+            vmem((width, hidden), BF16), vmem((hidden, width), BF16),
             vmem((width, hidden), BF16), vmem((hidden, width), BF16),
             vmem((width, hidden), BF16), vmem((hidden, width), BF16),
             vmem((16, 8, 128), F32),
             vmem(next_batch.shape, BF16), vmem(next_batch.shape, BF16), vmem(next_batch.shape, BF16),
             dma((10,)), dma((N_CHUNK,)), dma((N_CHUNK,)), dma((12,)), dma((12,)), dma((16,)), dma((16,)), dma((18,)), dma((18,)), dma((2,)), dma((2,)),
-            dma((n_micro,)), dma((n_micro,)), dma((n_micro,)), dma((n_micro,)),
+            dma((n_micro,)), dma((n_micro,)), dma((n_micro,)), dma((n_micro,)), dma((2,)), dma((2,)),
         ],
         compiler_params=pltpu.CompilerParams(collective_id=1, has_side_effects=True, vmem_limit_bytes=63 * 1024 * 1024),
     )(master_up, master_down, m1_up, m1_down, m2_up, m2_down, grad_up, grad_down, acts, loss_grad, next_batch, learn_rate, max_norm)
 
 
+def finish_kernel(outs_in, late_in, w_up_in, w_down_in, mean_up_in, mean_down_in, up_in, down_in, m1_up_in, m1_down_in, m2_up_in, m2_down_in, clip_ref, rate_ref,
+                  outs, up_out, down_out, m1_up_out, m1_down_out, m2_up_out, m2_down_out,
+                  obuf, late, w_up, w_down, upd_up, upd_down, load_sem, store_sem, micro_load, micro_store, late_load):
+    stage = lax.axis_index("stage")
+    n_micro = obuf.shape[0]
+    last = stage == 3
+    n_copied = jnp.where(last, n_micro - N_LATE, n_micro)
+    up_loads = [pltpu.make_async_copy(src, upd_up.at[i], load_sem.at[i]) for i, src in enumerate((mean_up_in, up_in, m1_up_in, m2_up_in))]
+    down_loads = [pltpu.make_async_copy(src, upd_down.at[i], load_sem.at[4 + i]) for i, src in enumerate((mean_down_in, down_in, m1_down_in, m2_down_in))]
+    w_loads = [pltpu.make_async_copy(w_up_in, w_up, load_sem.at[8]), pltpu.make_async_copy(w_down_in, w_down, load_sem.at[9])]
+    up_stores = [pltpu.make_async_copy(upd_up.at[1 + i], dst, store_sem.at[i]) for i, dst in enumerate((up_out, m1_up_out, m2_up_out))]
+    down_stores = [pltpu.make_async_copy(upd_down.at[1 + i], dst, store_sem.at[3 + i]) for i, dst in enumerate((down_out, m1_down_out, m2_down_out))]
+
+    def place(k):
+        return mixed(k, n_micro)[1]
+
+    def load_micro(k):
+        i = place(k)
+        return pltpu.make_async_copy(outs_in.at[i], obuf.at[i], micro_load.at[i])
+
+    def store_micro(k):
+        i = place(k)
+        return pltpu.make_async_copy(obuf.at[i], outs.at[i], micro_store.at[i])
+
+    def load_late(n):
+        return pltpu.make_async_copy(late_in.at[n], late.at[n], late_load.at[n])
+
+    for copy in up_loads:
+        copy.start()
+
+    def start_micro(k, _):
+        load_micro(k).start()
+        return 0
+
+    def turn_micro(k, _):
+        load_micro(k).wait()
+        store_micro(k).start()
+        return 0
+
+    @pl.when(last)
+    def _():
+        for copy in w_loads:
+            copy.start()
+        for n in range(N_LATE):
+            load_late(n).start()
+    for copy in down_loads:
+        copy.start()
+    lax.fori_loop(0, n_copied, start_micro, 0)
+    clip = clip_ref[0:1, 0:1]
+    rate = rate_ref[0]
+
+    def update(buf, n_rows):
+        def body(t, _):
+            rows = pl.ds(pl.multiple_of(t * n_rows, n_rows), n_rows)
+            new = adamw_update(buf[1, rows, :], buf[2, rows, :], buf[3, rows, :], buf[0, rows, :], clip, rate)
+            for i in range(3):
+                buf[1 + i, rows, :] = new[i]
+            return 0
+        lax.fori_loop(0, buf.shape[1] // n_rows, body, 0)
+
+    for copy in up_loads:
+        copy.wait()
+    update(upd_up, 32)
+    for copy in up_stores:
+        copy.start()
+    for copy in down_loads:
+        copy.wait()
+    update(upd_down, 128)
+    for copy in down_stores:
+        copy.start()
+
+    @pl.when(last)
+    def _():
+        for copy in w_loads:
+            copy.wait()
+
+        def body(n, _):
+            for j in range(3):
+                k = 3 * n + j
+
+                @pl.when(k < n_micro - N_LATE)
+                def _():
+                    turn_micro(k, 0)
+            load_late(n).wait()
+            k = n_micro - N_LATE + n
+            i = place(k)
+            stage_rows(late.at[n], w_up, w_down, obuf.at[i])
+            store_micro(k).start()
+            return 0
+        lax.fori_loop(0, N_LATE, body, 0)
+
+    @pl.when(jnp.logical_not(last))
+    def _():
+        lax.fori_loop(0, n_micro, turn_micro, 0)
+
+    def stored(k, _):
+        store_micro(k).wait()
+        return 0
+    lax.fori_loop(0, n_micro, stored, 0)
+    for copy in up_stores + down_stores:
+        copy.wait()
+
+
+def finish_step(outs, late, w_up, w_down, mean_up, mean_down, clip, master_up, master_down, m1_up, m1_down, m2_up, m2_down, learn_rate):
+    n_micro = outs.shape[0]
+    hbm = pl.BlockSpec(memory_space=pl.ANY)
+    vmem = pltpu.VMEM
+    dma = pltpu.SemaphoreType.DMA
+    up, down = jax.ShapeDtypeStruct(master_up.shape, F32), jax.ShapeDtypeStruct(master_down.shape, F32)
+    return pl.pallas_call(
+        finish_kernel,
+        name="finish_step",
+        out_shape=[jax.ShapeDtypeStruct(outs.shape, BF16), up, down, up, down, up, down],
+        in_specs=[hbm] * 12 + [pl.BlockSpec(memory_space=pltpu.VMEM), pl.BlockSpec(memory_space=pltpu.SMEM)],
+        out_specs=[hbm] * 7,
+        scratch_shapes=[
+            vmem(outs.shape, BF16), vmem(late.shape, BF16), vmem(w_up.shape, BF16), vmem(w_down.shape, BF16),
+            vmem((4,) + master_up.shape, F32), vmem((4,) + master_down.shape, F32),
+            dma((10,)), dma((6,)), dma((n_micro,)), dma((n_micro,)), dma((N_LATE,)),
+        ],
+        compiler_params=pltpu.CompilerParams(vmem_limit_bytes=56 * 1024 * 1024),
+    )(outs, late, w_up, w_down, mean_up, mean_down, master_up, master_down, m1_up, m1_down, m2_up, m2_down, clip, learn_rate)
+
+
 def solution(mesh):
     def local_step(master_up, master_down, mom1_up, mom1_down, mom2_up, mom2_down, grad_up, grad_down, stage_acts, loss_grad, next_batch, learn_rate, max_norm):
-        stage_outs, gbar_up, gbar_down, clip = fused_step(
+        stage_outs, gbar_up, gbar_down, clip, late, w_up, w_down = fused_step(
             master_up[0], master_down[0], mom1_up[0], mom1_down[0], mom2_up[0], mom2_down[0], grad_up[0, 0], grad_down[0, 0],
             stage_acts[0], loss_grad, next_batch, learn_rate.reshape(1), max_norm.reshape(1))
-        clip_scale = clip[0, 0]
-        new_up, new_m1_up, new_m2_up = adamw_update(master_up[0], mom1_up[0], mom2_up[0], gbar_up, clip_scale, learn_rate)
-        new_down, new_m1_down, new_m2_down = adamw_update(master_down[0], mom1_down[0], mom2_down[0], gbar_down, clip_scale, learn_rate)
+        stage_outs, new_up, new_down, new_m1_up, new_m1_down, new_m2_up, new_m2_down = finish_step(
+            stage_outs, late, w_up, w_down, gbar_up, gbar_down, clip, master_up[0], master_down[0], mom1_up[0], mom1_down[0], mom2_up[0], mom2_down[0], learn_rate.reshape(1))
         return (new_up[None], new_down[None], new_m1_up[None], new_m1_down[None], new_m2_up[None], new_m2_down[None], stage_outs[None])
 
     w_spec = P('stage', None, None)

time: 128 us -> 116 us (0.906)
  other arithmetic: 10.6 us -> 0 us
  local copies, waits for them, and re-layouts: 8.73 us -> 0 us
  Pallas kernels: 107 us -> 114 us
    pallas_call x0 -> x1, Pallas kernels: none -> 14.7 us  [finish_step(): pl.pallas_call(finish_kernel, name='finish_step', out_shape=[jax.ShapeDty...]
    broadcast_in_dim x2 -> x0, other arithmetic: 10.6 us -> none  [the longest x1 5.35 us: local_step(): new_m2_up[None]]
    unnamed x1 -> x0, local copies, waits for them, and re-layouts: 7.52 us -> none
    pallas_call x1, Pallas kernels: 107 us -> 99.6 us  [fused_step(): pl.pallas_call(step_kernel, name='pipeline_step', out_shape=[jax.ShapeDty...]
where the time goes in v3:
time: 116 us
  Pallas kernels  114 us (98%)
  between operations  2.1 us (2%)
    pallas_call x1, Pallas kernels, fused_step(): pl.pallas_call(step_kernel, name='pipeline_step', out_shape=[jax.ShapeDty...  99.6 us
    pallas_call x1, Pallas kernels, finish_step(): pl.pallas_call(finish_kernel, name='finish_step', out_shape=[jax.ShapeDty...  14.7 us

profile of v3, /device:TPU:3, one launch (start us, length us, event | category | flops | bytes accessed | tf_op | source)
XLA Modules:
  0.0 116.3 jit_solution(11562685579000049417)
XLA Ops:
  1.9 99.6 %pipeline_step.1 = (bf16[16,1024,256]{2,1,0:T(8,128)(2,1)}, f32[256,1024]{1,0:T(8,128)}, f32[1024,256]{1,0:T(8,128)}, f32[8,128]{1,0:T(8,128)}, bf16[5,1024,256]...) custom-call(f32[256,1024]{1,0:T(8,128)} %bitcast.21, f32[1024,256]{1,0:T(8,128)} %bitcast.23, ...), custom_call_target="tpu_custom_call" | custom-call | tf_op jit(solution)/shard_map/pipeline_step/pallas_call | solution.py:553
  101.5 14.7 %finish_step.1 = (bf16[16,1024,256]{2,1,0:T(8,128)(2,1)}, f32[256,1024]{1,0:T(8,128)}, f32[1024,256]{1,0:T(8,128)}, f32[256,1024]{1,0:T(8,128)}, f32[1024,256]{1...) custom-call(bf16[16,1024,256]{2,1,0:T(8,128)(2,1)} %get-tuple-element.21.outs_in, ...), custom_call_target="tpu_custom_call" | custom-call | tf_op jit(solution)/shard_map/finish_step/pallas_call | solution.py:691

commit v4 on v3

--- a/solution.py
+++ b/solution.py
@@ -16,8 +16,9 @@
 
 N_SENT = 6
 N_CHUNK = 4
-N_LATE = 5
-N_TWICE = 2
+N_LATE = 3
+N_TWICE = 1
+N_PIECE = 2
 MESH = pl.DeviceIdType.MESH
 BF16 = jnp.bfloat16
 F32 = jnp.float32
@@ -258,15 +259,13 @@
         pltpu.make_async_copy(m2_down_hbm, m_down.at[1], in_sem.at[8]),
     ]
     load_loss = pltpu.make_async_copy(loss_hbm, gbuf, in_sem.at[9])
-    loads[0].start()
-    loads[1].start()
+    for copy in loads[:2]:
+        copy.start()
 
     @pl.when(stage == 3)
     def _():
         load_loss.start()
-    for copy in loads[2:]:
-        copy.start()
-    start_loads(stage, nb_hbm, nbuf, nb_sem)
+    loads[2].start()
 
     barrier = pltpu.get_barrier_semaphore()
 
@@ -275,17 +274,6 @@
         pl.semaphore_signal(barrier, inc=1, device_id={"data": lax.div(other, 4), "stage": lax.rem(other, 4)}, device_id_type=MESH)
         return 0
     lax.fori_loop(1, 16, greet, 0)
-
-    loads[0].wait()
-    loads[1].wait()
-    up_bf[...] = up32[...].astype(BF16)
-    loads[2].wait()
-    down_bf[...] = down32[...].astype(BF16)
-    pl.semaphore_wait(barrier, 15)
-
-    @pl.when(stage == 3)
-    def _():
-        load_loss.wait()
 
     def chunk_rows(k):
         return pl.ds(pl.multiple_of(k * chunk, chunk), chunk)
@@ -320,48 +308,92 @@
             dxbuf[rows, :] = (grad.astype(F32) + mat_nt(d_pre, up_bf[...])).astype(BF16)
             pass_down(k).start()
 
+    def rs_copy(src, dst, sem, peer):
+        return pltpu.make_async_remote_copy(src_ref=src, dst_ref=dst, send_sem=rs_send.at[sem], recv_sem=rs_recv.at[sem], device_id={"data": peer}, device_id_type=MESH)
+
+    def v_first(sub, c):
+        yy = (1 - y) if sub == 0 else y
+        return rs_copy(gv.at[down_rows(1 - z, yy, 128 * c, 128)], rv1.at[sub, pl.ds(128 * c, 128)], 2 * sub + c, z_peer)
+
+    def u_first(sub, c):
+        zz = (1 - z) if sub == 0 else z
+        return rs_copy(gu.at[up_rows(zz, 1 - y, 32 * c, 32)], ru1.at[sub, pl.ds(32 * c, 32)], 4 + 2 * sub + c, y_peer)
+
+    def v_second(c):
+        return rs_copy(gv.at[down_rows(z, 1 - y, 128 * c, 128)], rv2.at[pl.ds(128 * c, 128)], 8 + c, y_peer)
+
+    def u_second(c):
+        return rs_copy(gu.at[up_rows(1 - z, y, 32 * c, 32)], ru2.at[pl.ds(32 * c, 32)], 10 + c, z_peer)
+
+    def add_grads(k):
+        rows = chunk_rows(k)
+
+        @pl.when(k == 0)
+        def _():
+            loads[3].wait()
+            loads[4].wait()
+
+        def half(h, _):
+            zz = h * z + (1 - h) * (1 - z)
+            yy = h * y + (1 - h) * (1 - y)
+            send = (k == N_CHUNK - 1) & (h == 0)
+            out = pl.ds(pl.multiple_of(512 * zz, 512), 512)
+            gv[out, :] += mat_tn(hid[rows, out], gbuf[rows, :])
+
+            @pl.when(send)
+            def _():
+                for sub in range(2):
+                    for c in range(2):
+                        v_first(sub, c).start()
+            out = pl.ds(pl.multiple_of(128 * yy, 128), 128)
+            gu[out, :] += mat_tn(acts[rows, out], dpre[rows, :])
+
+            @pl.when(send)
+            def _():
+                for sub in range(2):
+                    for c in range(2):
+                        u_first(sub, c).start()
+            return 0
+        lax.fori_loop(0, 2, half, 0)
+
     def tick(t, _):
         upper = jnp.where(stage >= 2, 1, 0)
-        is_prep = upper * (1 - lax.rem(t, 2)) + (1 - upper) * (1 - lax.div(t, N_CHUNK))
-        k = upper * lax.div(t, 2) + (1 - upper) * lax.rem(t, N_CHUNK)
+        even = 1 - lax.rem(t, 2)
+        early = jnp.where(t < N_CHUNK, 1, 0)
+        late = jnp.where(t >= 2 * N_CHUNK, 1, 0)
+        is_prep = upper * even * (1 - late) + (1 - upper) * early
+        is_grad = upper * late + (1 - upper) * (1 - early) * (1 - even)
+        k = upper * (late * (t - 2 * N_CHUNK) + (1 - late) * lax.div(t, 2)) + (1 - upper) * (early * t + (1 - early) * lax.div(t - N_CHUNK, 2))
 
         @pl.when(is_prep == 1)
         def _():
             prepare(k)
 
-        @pl.when(is_prep == 0)
+        @pl.when(is_prep + is_grad == 0)
         def _():
             backward(k)
-        return 0
-    lax.fori_loop(0, 2 * N_CHUNK, tick, 0)
-
-    def rs_copy(src, dst, sem, peer):
-        return pltpu.make_async_remote_copy(src_ref=src, dst_ref=dst, send_sem=rs_send.at[sem], recv_sem=rs_recv.at[sem], device_id={"data": peer}, device_id_type=MESH)
-
-    def v_first(sub, c):
-        yy = (1 - y) if sub == 0 else y
-        return rs_copy(gv.at[down_rows(1 - z, yy, 128 * c, 128)], rv1.at[sub, pl.ds(128 * c, 128)], 2 * sub + c, z_peer)
-
-    def u_first(sub, c):
-        zz = (1 - z) if sub == 0 else z
-        return rs_copy(gu.at[up_rows(zz, 1 - y, 32 * c, 32)], ru1.at[sub, pl.ds(32 * c, 32)], 4 + 2 * sub + c, y_peer)
-
-    def v_second(c):
-        return rs_copy(gv.at[down_rows(z, 1 - y, 128 * c, 128)], rv2.at[pl.ds(128 * c, 128)], 8 + c, y_peer)
-
-    def u_second(c):
-        return rs_copy(gu.at[up_rows(1 - z, y, 32 * c, 32)], ru2.at[pl.ds(32 * c, 32)], 10 + c, z_peer)
-
-    loads[3].wait()
-    gv[...] += mat_tn(hid[...], gbuf[...])
-    for sub in range(2):
-        for c in range(2):
-            v_first(sub, c).start()
-    loads[4].wait()
-    gu[...] += mat_tn(acts[...], dpre[...])
-    for sub in range(2):
-        for c in range(2):
-            u_first(sub, c).start()
+
+        @pl.when(is_grad == 1)
+        def _():
+            add_grads(k)
+        return 0
+
+    loads[0].wait()
+    loads[1].wait()
+    up_bf[...] = up32[...].astype(BF16)
+    prepare(0)
+    loads[2].wait()
+    for copy in loads[3:]:
+        copy.start()
+    start_loads(stage, nb_hbm, nbuf, nb_sem)
+    down_bf[...] = down32[...].astype(BF16)
+    pl.semaphore_wait(barrier, 15)
+
+    @pl.when(stage == 3)
+    def _():
+        load_loss.wait()
+    lax.fori_loop(1, 3 * N_CHUNK, tick, 0)
+
     for c in range(2):
         v_first(0, c).wait_recv()
         rows = down_rows(z, 1 - y, 128 * c, 128)
@@ -394,33 +426,52 @@
         mean_up[rows, :] = mean
         acc = fold(mean, acc)
 
+    up_piece, down_piece = 64 // N_PIECE, 256 // N_PIECE
+
     def gather(which, up, down):
-        def copy(ref, rows, sem, peer):
-            return pltpu.make_async_remote_copy(src_ref=ref.at[rows], dst_ref=ref.at[rows], send_sem=ag_send.at[which * 6 + sem], recv_sem=ag_recv.at[which * 6 + sem],
+        def copy(ref, rows, sem, piece, peer):
+            sem = (which * 6 + sem) * N_PIECE + piece
+            return pltpu.make_async_remote_copy(src_ref=ref.at[rows], dst_ref=ref.at[rows], send_sem=ag_send.at[sem], recv_sem=ag_recv.at[sem],
                                                 device_id={"data": peer}, device_id_type=MESH)
 
-        sends = [copy(up, own_up, 0, z_peer), copy(down, own_down, 3, y_peer), copy(up, own_up, 1, y_peer), copy(down, own_down, 4, z_peer)]
-        relays = [copy(up, up_rows(1 - z, y), 2, y_peer), copy(down, down_rows(z, 1 - y), 5, z_peer)]
-        arrive_first = [copy(up, up_rows(1 - z, y), 0, z_peer), copy(down, down_rows(z, 1 - y), 3, y_peer)]
-        arrive_rest = [copy(up, up_rows(z, 1 - y), 1, y_peer), copy(down, down_rows(1 - z, y), 4, z_peer),
-                       copy(up, up_rows(1 - z, 1 - y), 2, y_peer), copy(down, down_rows(1 - z, 1 - y), 5, z_peer)]
-
-        def begin():
-            for c in sends:
-                c.start()
+        def up_copy(zz, yy, sem, p, peer):
+            return copy(up, up_rows(zz, yy, up_piece * p, up_piece), sem, p, peer)
+
+        def down_copy(zz, yy, sem, p, peer):
+            return copy(down, down_rows(zz, yy, down_piece * p, down_piece), sem, p, peer)
+
+        def up_sends(p):
+            return [up_copy(z, y, 0, p, z_peer), up_copy(z, y, 1, p, y_peer)]
+
+        def down_sends(p):
+            return [down_copy(z, y, 3, p, y_peer), down_copy(z, y, 4, p, z_peer)]
+
+        def relays(p):
+            return [(up_copy(1 - z, y, 0, p, z_peer), up_copy(1 - z, y, 2, p, y_peer)), (down_copy(z, 1 - y, 3, p, y_peer), down_copy(z, 1 - y, 5, p, z_peer))]
+
+        def begin(fed=None):
+            for p in range(N_PIECE):
+                for i, sends in enumerate((up_sends(p), down_sends(p))):
+                    if fed is not None:
+                        fed(p)[i].wait_recv()
+                    for c in sends:
+                        c.start()
 
         def relay():
-            for a, c in zip(arrive_first, relays):
-                a.wait_recv()
-                c.start()
+            for p in range(N_PIECE):
+                for arrived, onward in relays(p):
+                    arrived.wait_recv()
+                    onward.start()
 
         def finish():
-            for c in arrive_rest:
-                c.wait_recv()
+            for p in range(N_PIECE):
+                for c in (up_copy(z, 1 - y, 1, p, y_peer), down_copy(1 - z, y, 4, p, z_peer), up_copy(1 - z, 1 - y, 2, p, y_peer), down_copy(1 - z, 1 - y, 5, p, z_peer)):
+                    c.wait_recv()
 
         def drain():
-            for c in sends + relays:
-                c.wait_send()
+            for p in range(N_PIECE):
+                for c in up_sends(p) + down_sends(p) + [onward for _, onward in relays(p)]:
+                    c.wait_send()
         return begin, relay, finish, drain
 
     own_begin, own_relay, own_finish, own_drain = gather(0, up_own, down_own)
@@ -471,24 +522,23 @@
         return 0
     lax.fori_loop(0, 1 + 3 * whole, renew, 0)
 
-    def feed():
-        peer = 3 - stage
-        return [pltpu.make_async_remote_copy(src_ref=own.at[rows], dst_ref=aux.at[rows], send_sem=aux_send.at[i], recv_sem=aux_recv.at[i], device_id={"stage": peer}, device_id_type=MESH)
-                for i, (own, aux, rows) in enumerate([(up_own, up_aux, own_up), (down_own, down_aux, own_down)])]
+    def feed(p):
+        parts = [(up_own, up_aux, up_rows(z, y, up_piece * p, up_piece)), (down_own, down_aux, down_rows(z, y, down_piece * p, down_piece))]
+        return [pltpu.make_async_remote_copy(src_ref=own.at[rows], dst_ref=aux.at[rows], send_sem=aux_send.at[2 * p + i], recv_sem=aux_recv.at[2 * p + i], device_id={"stage": 3 - stage}, device_id_type=MESH)
+                for i, (own, aux, rows) in enumerate(parts)]
 
     @pl.when(stage < 2)
     def _():
-        for c in feed():
-            c.start()
+        for p in range(N_PIECE):
+            for c in feed(p):
+                c.start()
         own_begin()
         own_relay()
         mean_begin()
 
     @pl.when(stage >= 2)
     def _():
-        for c in feed():
-            c.wait_recv()
-        aux_begin()
+        aux_begin(feed)
         aux_relay()
 
     def relay_mean(now):
@@ -530,8 +580,9 @@
     @pl.when(stage < 2)
     def _():
         own_drain()
-        for c in feed():
-            c.wait_send()
+        for p in range(N_PIECE):
+            for c in feed(p):
+                c.wait_send()
 
     @pl.when(stage >= 2)
     def _():
@@ -572,7 +623,7 @@
             vmem((width, hidden), BF16), vmem((hidden, width), BF16),
             vmem((16, 8, 128), F32),
             vmem(next_batch.shape, BF16), vmem(next_batch.shape, BF16), vmem(next_batch.shape, BF16),
-            dma((10,)), dma((N_CHUNK,)), dma((N_CHUNK,)), dma((12,)), dma((12,)), dma((16,)), dma((16,)), dma((18,)), dma((18,)), dma((2,)), dma((2,)),
+            dma((10,)), dma((N_CHUNK,)), dma((N_CHUNK,)), dma((12,)), dma((12,)), dma((16,)), dma((16,)), dma((18 * N_PIECE,)), dma((18 * N_PIECE,)), dma((2 * N_PIECE,)), dma((2 * N_PIECE,)),
             dma((n_micro,)), dma((n_micro,)), dma((n_micro,)), dma((n_micro,)), dma((2,)), dma((2,)),
         ],
         compiler_params=pltpu.CompilerParams(collective_id=1, has_side_effects=True, vmem_limit_bytes=63 * 1024 * 1024),
@@ -586,6 +637,7 @@
     n_micro = obuf.shape[0]
     last = stage == 3
     n_copied = jnp.where(last, n_micro - N_LATE, n_micro)
+    per_late = -(-(n_micro - N_LATE) // N_LATE)
     up_loads = [pltpu.make_async_copy(src, upd_up.at[i], load_sem.at[i]) for i, src in enumerate((mean_up_in, up_in, m1_up_in, m2_up_in))]
     down_loads = [pltpu.make_async_copy(src, upd_down.at[i], load_sem.at[4 + i]) for i, src in enumerate((mean_down_in, down_in, m1_down_in, m2_down_in))]
     w_loads = [pltpu.make_async_copy(w_up_in, w_up, load_sem.at[8]), pltpu.make_async_copy(w_down_in, w_down, load_sem.at[9])]
@@ -656,8 +708,8 @@
             copy.wait()
 
         def body(n, _):
-            for j in range(3):
-                k = 3 * n + j
+            for j in range(per_late):
+                k = per_late * n + j
 
                 @pl.when(k < n_micro - N_LATE)
                 def _():

time: 116 us -> 118 us (1.017)
  Pallas kernels: 114 us -> 116 us
    pallas_call x1, Pallas kernels: 99.6 us -> 103 us  [fused_step(): pl.pallas_call(step_kernel, name='pipeline_step', out_shape=[jax.ShapeDty...]
    pallas_call x1, Pallas kernels: 14.7 us -> 12.9 us  [finish_step(): pl.pallas_call(finish_kernel, name='finish_step', out_shape=[jax.ShapeDty...]
where the time goes in v4:
time: 118 us
  Pallas kernels  116 us (98%)
  between operations  2.1 us (2%)
    pallas_call x1, Pallas kernels, fused_step(): pl.pallas_call(step_kernel, name='pipeline_step', out_shape=[jax.ShapeDty...  103 us
    pallas_call x1, Pallas kernels, finish_step(): pl.pallas_call(finish_kernel, name='finish_step', out_shape=[jax.ShapeDty...  12.9 us

profile of v4, /device:TPU:3, one launch (start us, length us, event | category | flops | bytes accessed | tf_op | source)
XLA Modules:
  0.0 118.2 jit_solution(7611073322945872632)
XLA Ops:
  1.9 103.1 %pipeline_step.1 = (bf16[16,1024,256]{2,1,0:T(8,128)(2,1)}, f32[256,1024]{1,0:T(8,128)}, f32[1024,256]{1,0:T(8,128)}, f32[8,128]{1,0:T(8,128)}, bf16[3,1024,256]...) custom-call(f32[256,1024]{1,0:T(8,128)} %bitcast.21, f32[1024,256]{1,0:T(8,128)} %bitcast.23, ...), custom_call_target="tpu_custom_call" | custom-call | tf_op jit(solution)/shard_map/pipeline_step/pallas_call | solution.py:604
  105.1 12.9 %finish_step.1 = (bf16[16,1024,256]{2,1,0:T(8,128)(2,1)}, f32[256,1024]{1,0:T(8,128)}, f32[1024,256]{1,0:T(8,128)}, f32[256,1024]{1,0:T(8,128)}, f32[1024,256]{1...) custom-call(bf16[16,1024,256]{2,1,0:T(8,128)(2,1)} %get-tuple-element.21.outs_in, ...), custom_call_target="tpu_custom_call" | custom-call | tf_op jit(solution)/shard_map/finish_step/pallas_call | solution.py:743

commit v5 on v4

--- a/solution.py
+++ b/solution.py
@@ -16,9 +16,9 @@
 
 N_SENT = 6
 N_CHUNK = 4
-N_LATE = 3
-N_TWICE = 1
-N_PIECE = 2
+N_LATE = 6
+N_TWICE = 3
+N_PIECE = 1
 MESH = pl.DeviceIdType.MESH
 BF16 = jnp.bfloat16
 F32 = jnp.float32
@@ -225,7 +225,7 @@
 
 
 def step_kernel(up_hbm, down_hbm, m1_up_hbm, m1_down_hbm, m2_up_hbm, m2_down_hbm, gu_hbm, gv_hbm, acts_hbm, loss_hbm, nb_hbm, rate_ref, norm_ref,
-                out_hbm, mean_up_hbm, mean_down_hbm, clip_out, late_hbm, w_up_hbm, w_down_hbm,
+                out_hbm, new_up_hbm, new_down_hbm, new_m1_up_hbm, new_m1_down_hbm, new_m2_up_hbm, new_m2_down_hbm, late_hbm, w_up_hbm, w_down_hbm,
                 up32, down32, gu, gv, mean_up, mean_down, acts, gbuf, dxbuf, hid, slope, dpre, up_bf, down_bf,
                 ru1, rv1, ru2, rv2, m_up, m_down, up_own, down_own, up_aux, down_aux, up_two, down_two, sq_all, nbuf, xin, yout,
                 in_sem, g_send, g_recv, rs_send, rs_recv, sq_send, sq_recv, ag_send, ag_recv, aux_send, aux_recv,
@@ -507,20 +507,36 @@
         total = total + sq_all[i]
     total = jnp.sum(jnp.sum(total, axis=0, keepdims=True), axis=1, keepdims=True)
     clip = jnp.minimum(1.0, norm_ref[0] / (jnp.sqrt(total) + NORM_EPS))
-    clip_out[...] = jnp.broadcast_to(clip, clip_out.shape)
 
     rate = rate_ref[0]
     whole = jnp.where(stage >= 2, 1, 0)
 
-    def renew(t, _):
-        rows = pl.ds(pl.multiple_of(64 * (whole * t + (1 - whole) * (2 * y + z)), 64), 64)
-        new_up, _, _ = adamw_update(up32[rows, :], m_up[0, rows, :], m_up[1, rows, :], mean_up[rows, :], clip, rate)
-        up_own[rows, :] = new_up.astype(BF16) * jnp.asarray(0.5, BF16)
-        rows = pl.ds(pl.multiple_of(256 * (whole * t + (1 - whole) * (2 * z + y)), 256), 256)
-        new_down, _, _ = adamw_update(down32[rows, :], m_down[0, rows, :], m_down[1, rows, :], mean_down[rows, :], clip, rate)
-        down_own[rows, :] = new_down.astype(BF16)
-        return 0
-    lax.fori_loop(0, 1 + 3 * whole, renew, 0)
+    def renew(rows, master, moments, mean, weights, scale, first, full):
+        new = adamw_update(master[rows, :], moments[0, rows, :], moments[1, rows, :], mean[rows, :], clip, rate)
+        if first:
+            weights[rows, :] = new[0].astype(BF16) * jnp.asarray(scale, BF16)
+
+        @pl.when(full)
+        def _():
+            master[rows, :] = new[0]
+            moments[0, rows, :] = new[1]
+            moments[1, rows, :] = new[2]
+
+    def renew_block(up_block, down_block, first, full):
+        renew(pl.ds(pl.multiple_of(64 * up_block, 64), 64), up32, m_up, mean_up, up_own, 0.5, first, full)
+        renew(pl.ds(pl.multiple_of(256 * down_block, 256), 256), down32, m_down, mean_down, down_own, 1.0, first, full)
+
+    def renew_first(t, _):
+        renew_block(whole * t + (1 - whole) * (2 * y + z), whole * t + (1 - whole) * (2 * z + y), True, whole == 1)
+        return 0
+
+    def renew_rest(t, _):
+        renew_block(t, t, False, t >= 0)
+        return 0
+
+    new_stores = [pltpu.make_async_copy(src, dst, in_sem.at[i]) for i, (src, dst) in enumerate((
+        (up32, new_up_hbm), (down32, new_down_hbm), (m_up.at[0], new_m1_up_hbm), (m_down.at[0], new_m1_down_hbm), (m_up.at[1], new_m2_up_hbm), (m_down.at[1], new_m2_down_hbm)))]
+    lax.fori_loop(0, 1 + 3 * whole, renew_first, 0)
 
     def feed(p):
         parts = [(up_own, up_aux, up_rows(z, y, up_piece * p, up_piece)), (down_own, down_aux, down_rows(z, y, down_piece * p, down_piece))]
@@ -538,6 +554,8 @@
 
     @pl.when(stage >= 2)
     def _():
+        for copy in new_stores:
+            copy.start()
         aux_begin(feed)
         aux_relay()
 
@@ -551,12 +569,11 @@
     @pl.when(stage < 2)
     def _():
         mean_finish()
-    store_up = pltpu.make_async_copy(mean_up, mean_up_hbm, in_sem.at[0])
-    store_down = pltpu.make_async_copy(mean_down, mean_down_hbm, in_sem.at[1])
-    store_w_up = pltpu.make_async_copy(up_own, w_up_hbm, in_sem.at[2])
-    store_w_down = pltpu.make_async_copy(down_own, w_down_hbm, in_sem.at[3])
-    store_up.start()
-    store_down.start()
+        lax.fori_loop(0, 4, renew_rest, 0)
+        for copy in new_stores:
+            copy.start()
+    store_w_up = pltpu.make_async_copy(up_own, w_up_hbm, in_sem.at[6])
+    store_w_down = pltpu.make_async_copy(down_own, w_down_hbm, in_sem.at[7])
     store_w_up.start()
     store_w_down.start()
 
@@ -587,8 +604,8 @@
     @pl.when(stage >= 2)
     def _():
         aux_drain()
-    store_up.wait()
-    store_down.wait()
+    for copy in new_stores:
+        copy.wait()
     store_w_up.wait()
     store_w_down.wait()
 
@@ -604,10 +621,10 @@
     return pl.pallas_call(
         step_kernel,
         name="pipeline_step",
-        out_shape=[jax.ShapeDtypeStruct(next_batch.shape, BF16), jax.ShapeDtypeStruct((width, hidden), F32), jax.ShapeDtypeStruct((hidden, width), F32), jax.ShapeDtypeStruct((8, 128), F32),
-                   jax.ShapeDtypeStruct((N_LATE,) + next_batch.shape[1:], BF16), jax.ShapeDtypeStruct((width, hidden), BF16), jax.ShapeDtypeStruct((hidden, width), BF16)],
+        out_shape=[jax.ShapeDtypeStruct(next_batch.shape, BF16)] + [jax.ShapeDtypeStruct((width, hidden), F32), jax.ShapeDtypeStruct((hidden, width), F32)] * 3 + [
+            jax.ShapeDtypeStruct((N_LATE,) + next_batch.shape[1:], BF16), jax.ShapeDtypeStruct((width, hidden), BF16), jax.ShapeDtypeStruct((hidden, width), BF16)],
         in_specs=[hbm] * 11 + [smem] * 2,
-        out_specs=[hbm, hbm, hbm, pl.BlockSpec(memory_space=pltpu.VMEM), hbm, hbm, hbm],
+        out_specs=[hbm] * 10,
         scratch_shapes=[
             vmem((width, hidden), F32), vmem((hidden, width), F32),
             vmem((width, hidden), F32), vmem((hidden, width), F32),
@@ -630,19 +647,18 @@
     )(master_up, master_down, m1_up, m1_down, m2_up, m2_down, grad_up, grad_down, acts, loss_grad, next_batch, learn_rate, max_norm)
 
 
-def finish_kernel(outs_in, late_in, w_up_in, w_down_in, mean_up_in, mean_down_in, up_in, down_in, m1_up_in, m1_down_in, m2_up_in, m2_down_in, clip_ref, rate_ref,
-                  outs, up_out, down_out, m1_up_out, m1_down_out, m2_up_out, m2_down_out,
-                  obuf, late, w_up, w_down, upd_up, upd_down, load_sem, store_sem, micro_load, micro_store, late_load):
+def finish_kernel(outs_in, late_in, w_up_in, w_down_in, *refs):
+    news_in, outs, news_out = refs[:6], refs[6], refs[7:13]
+    obuf, late, w_up, w_down, upd_up, upd_down, load_sem, store_sem, micro_load, micro_store, late_load = refs[13:]
     stage = lax.axis_index("stage")
     n_micro = obuf.shape[0]
     last = stage == 3
     n_copied = jnp.where(last, n_micro - N_LATE, n_micro)
     per_late = -(-(n_micro - N_LATE) // N_LATE)
-    up_loads = [pltpu.make_async_copy(src, upd_up.at[i], load_sem.at[i]) for i, src in enumerate((mean_up_in, up_in, m1_up_in, m2_up_in))]
-    down_loads = [pltpu.make_async_copy(src, upd_down.at[i], load_sem.at[4 + i]) for i, src in enumerate((mean_down_in, down_in, m1_down_in, m2_down_in))]
-    w_loads = [pltpu.make_async_copy(w_up_in, w_up, load_sem.at[8]), pltpu.make_async_copy(w_down_in, w_down, load_sem.at[9])]
-    up_stores = [pltpu.make_async_copy(upd_up.at[1 + i], dst, store_sem.at[i]) for i, dst in enumerate((up_out, m1_up_out, m2_up_out))]
-    down_stores = [pltpu.make_async_copy(upd_down.at[1 + i], dst, store_sem.at[3 + i]) for i, dst in enumerate((down_out, m1_down_out, m2_down_out))]
+    slots = [buf.at[i] for i in range(3) for buf in (upd_up, upd_down)]
+    loads = [pltpu.make_async_copy(src, slot, load_sem.at[i]) for i, (src, slot) in enumerate(zip(news_in, slots))]
+    stores = [pltpu.make_async_copy(slot, dst, store_sem.at[i]) for i, (slot, dst) in enumerate(zip(slots, news_out))]
+    w_loads = [pltpu.make_async_copy(w_up_in, w_up, load_sem.at[6]), pltpu.make_async_copy(w_down_in, w_down, load_sem.at[7])]
 
     def place(k):
         return mixed(k, n_micro)[1]
@@ -658,9 +674,6 @@
     def load_late(n):
         return pltpu.make_async_copy(late_in.at[n], late.at[n], late_load.at[n])
 
-    for copy in up_loads:
-        copy.start()
-
     def start_micro(k, _):
         load_micro(k).start()
         return 0
@@ -670,37 +683,18 @@
         store_micro(k).start()
         return 0
 
+    def start_late(n, _):
+        load_late(n).start()
+        return 0
+
     @pl.when(last)
     def _():
         for copy in w_loads:
             copy.start()
-        for n in range(N_LATE):
-            load_late(n).start()
-    for copy in down_loads:
+        lax.fori_loop(0, N_LATE, start_late, 0)
+    for copy in loads:
         copy.start()
     lax.fori_loop(0, n_copied, start_micro, 0)
-    clip = clip_ref[0:1, 0:1]
-    rate = rate_ref[0]
-
-    def update(buf, n_rows):
-        def body(t, _):
-            rows = pl.ds(pl.multiple_of(t * n_rows, n_rows), n_rows)
-            new = adamw_update(buf[1, rows, :], buf[2, rows, :], buf[3, rows, :], buf[0, rows, :], clip, rate)
-            for i in range(3):
-                buf[1 + i, rows, :] = new[i]
-            return 0
-        lax.fori_loop(0, buf.shape[1] // n_rows, body, 0)
-
-    for copy in up_loads:
-        copy.wait()
-    update(upd_up, 32)
-    for copy in up_stores:
-        copy.start()
-    for copy in down_loads:
-        copy.wait()
-    update(upd_down, 128)
-    for copy in down_stores:
-        copy.start()
 
     @pl.when(last)
     def _():
@@ -708,60 +702,66 @@
             copy.wait()
 
         def body(n, _):
+            load_late(n).wait()
+            k = n_micro - N_LATE + n
+            stage_rows(late.at[n], w_up, w_down, obuf.at[place(k)])
+            store_micro(k).start()
+
+            @pl.when(n == 0)
+            def _():
+                for load, store in zip(loads, stores):
+                    load.wait()
+                    store.start()
             for j in range(per_late):
                 k = per_late * n + j
 
                 @pl.when(k < n_micro - N_LATE)
                 def _():
                     turn_micro(k, 0)
-            load_late(n).wait()
-            k = n_micro - N_LATE + n
-            i = place(k)
-            stage_rows(late.at[n], w_up, w_down, obuf.at[i])
-            store_micro(k).start()
             return 0
         lax.fori_loop(0, N_LATE, body, 0)
 
     @pl.when(jnp.logical_not(last))
     def _():
+        for load, store in zip(loads, stores):
+            load.wait()
+            store.start()
         lax.fori_loop(0, n_micro, turn_micro, 0)
 
     def stored(k, _):
         store_micro(k).wait()
         return 0
     lax.fori_loop(0, n_micro, stored, 0)
-    for copy in up_stores + down_stores:
+    for copy in stores:
         copy.wait()
 
 
-def finish_step(outs, late, w_up, w_down, mean_up, mean_down, clip, master_up, master_down, m1_up, m1_down, m2_up, m2_down, learn_rate):
+def finish_step(outs, late, w_up, w_down, *news):
     n_micro = outs.shape[0]
     hbm = pl.BlockSpec(memory_space=pl.ANY)
     vmem = pltpu.VMEM
     dma = pltpu.SemaphoreType.DMA
-    up, down = jax.ShapeDtypeStruct(master_up.shape, F32), jax.ShapeDtypeStruct(master_down.shape, F32)
     return pl.pallas_call(
         finish_kernel,
         name="finish_step",
-        out_shape=[jax.ShapeDtypeStruct(outs.shape, BF16), up, down, up, down, up, down],
-        in_specs=[hbm] * 12 + [pl.BlockSpec(memory_space=pltpu.VMEM), pl.BlockSpec(memory_space=pltpu.SMEM)],
+        out_shape=[jax.ShapeDtypeStruct(outs.shape, BF16)] + [jax.ShapeDtypeStruct(new.shape, F32) for new in news],
+        in_specs=[hbm] * 10,
         out_specs=[hbm] * 7,
         scratch_shapes=[
             vmem(outs.shape, BF16), vmem(late.shape, BF16), vmem(w_up.shape, BF16), vmem(w_down.shape, BF16),
-            vmem((4,) + master_up.shape, F32), vmem((4,) + master_down.shape, F32),
-            dma((10,)), dma((6,)), dma((n_micro,)), dma((n_micro,)), dma((N_LATE,)),
+            vmem((3,) + news[0].shape, F32), vmem((3,) + news[1].shape, F32),
+            dma((8,)), dma((6,)), dma((n_micro,)), dma((n_micro,)), dma((N_LATE,)),
         ],
         compiler_params=pltpu.CompilerParams(vmem_limit_bytes=56 * 1024 * 1024),
-    )(outs, late, w_up, w_down, mean_up, mean_down, master_up, master_down, m1_up, m1_down, m2_up, m2_down, clip, learn_rate)
+    )(outs, late, w_up, w_down, *news)
 
 
 def solution(mesh):
     def local_step(master_up, master_down, mom1_up, mom1_down, mom2_up, mom2_down, grad_up, grad_down, stage_acts, loss_grad, next_batch, learn_rate, max_norm):
-        stage_outs, gbar_up, gbar_down, clip, late, w_up, w_down = fused_step(
+        stage_outs, *news, late, w_up, w_down = fused_step(
             master_up[0], master_down[0], mom1_up[0], mom1_down[0], mom2_up[0], mom2_down[0], grad_up[0, 0], grad_down[0, 0],
             stage_acts[0], loss_grad, next_batch, learn_rate.reshape(1), max_norm.reshape(1))
-        stage_outs, new_up, new_down, new_m1_up, new_m1_down, new_m2_up, new_m2_down = finish_step(
-            stage_outs, late, w_up, w_down, gbar_up, gbar_down, clip, master_up[0], master_down[0], mom1_up[0], mom1_down[0], mom2_up[0], mom2_down[0], learn_rate.reshape(1))
+        stage_outs, new_up, new_down, new_m1_up, new_m1_down, new_m2_up, new_m2_down = finish_step(stage_outs, late, w_up, w_down, *news)
         return (new_up[None], new_down[None], new_m1_up[None], new_m1_down[None], new_m2_up[None], new_m2_down[None], stage_outs[None])
 
     w_spec = P('stage', None, None)

time: 118 us -> 118 us (level)
    pallas_call x1, Pallas kernels: 103 us -> 101 us  [fused_step(): pl.pallas_call(step_kernel, name='pipeline_step', out_shape=[jax.ShapeDty...]
    pallas_call x1, Pallas kernels: 12.9 us -> 14.2 us  [finish_step(): pl.pallas_call(finish_kernel, name='finish_step', out_shape=[jax.ShapeDty...]
where the time goes in v5:
time: 118 us; the launch traced here: 117 us
  Pallas kernels  115 us (97%)
  between operations  2.1 us (2%)
    pallas_call x1, Pallas kernels, fused_step(): pl.pallas_call(step_kernel, name='pipeline_step', out_shape=[jax.ShapeDty...  101 us
    pallas_call x1, Pallas kernels, finish_step(): pl.pallas_call(finish_kernel, name='finish_step', out_shape=[jax.ShapeDty...  14.2 us

profile of v5, /device:TPU:3, one launch (start us, length us, event | category | flops | bytes accessed | tf_op | source)
XLA Modules:
  0.0 117.1 jit_solution(11248623889311067453)
XLA Ops:
  1.9 100.8 %pipeline_step.1 = (bf16[16,1024,256]{2,1,0:T(8,128)(2,1)}, f32[256,1024]{1,0:T(8,128)}, f32[1024,256]{1,0:T(8,128)}, f32[256,1024]{1,0:T(8,128)}, f32[1024,256]...) custom-call(f32[256,1024]{1,0:T(8,128)} %bitcast.20, ...), custom_call_target="tpu_custom_call" | custom-call | tf_op jit(solution)/shard_map/pipeline_step/pallas_call | solution.py:621
  102.8 14.2 %finish_step.1 = (bf16[16,1024,256]{2,1,0:T(8,128)(2,1)}, f32[256,1024]{1,0:T(8,128)}, f32[1024,256]{1,0:T(8,128)}, f32[256,1024]{1,0:T(8,128)}, f32[1024,256]{1...) custom-call(bf16[16,1024,256]{2,1,0:T(8,128)(2,1)} %get-tuple-element.24.outs_in, ...), custom_call_target="tpu_custom_call" | custom-call | tf_op jit(solution)/shard_map/finish_step/pallas_call | solution.py:744

commit v6 on v5

--- a/solution.py
+++ b/solution.py
@@ -14,7 +14,7 @@
 SQRT_TWO_PI = 0.7978845608028654
 GELU_CUBIC = 0.044715
 
-N_SENT = 6
+N_SENT = 5
 N_CHUNK = 4
 N_LATE = 6
 N_TWICE = 3
@@ -128,7 +128,6 @@
             relay_mean(j == 7)
             return 0
         lax.fori_loop(0, n_micro, body, 0)
-        finish_sends(n_kept, N_SENT)
         finish_stores()
 
     @pl.when(stage == 2)
@@ -576,6 +575,13 @@
     store_w_down = pltpu.make_async_copy(down_own, w_down_hbm, in_sem.at[7])
     store_w_up.start()
     store_w_down.start()
+
+    @pl.when(stage == 1)
+    def _():
+        def left(i, _):
+            pltpu.make_async_remote_copy(src_ref=yout.at[i], dst_ref=xin.at[i], send_sem=send_sem.at[i], recv_sem=recv_sem.at[i], device_id={"stage": 2}, device_id_type=MESH).wait_send()
+            return 0
+        lax.fori_loop(nbuf.shape[0] - N_SENT, nbuf.shape[0], left, 0)
 
     @pl.when(stage > 0)
     def _():
@@ -654,7 +660,7 @@
     n_micro = obuf.shape[0]
     last = stage == 3
     n_copied = jnp.where(last, n_micro - N_LATE, n_micro)
-    per_late = -(-(n_micro - N_LATE) // N_LATE)
+    per_late = -(-(n_micro - N_LATE) // (N_LATE - 2))
     slots = [buf.at[i] for i in range(3) for buf in (upd_up, upd_down)]
     loads = [pltpu.make_async_copy(src, slot, load_sem.at[i]) for i, (src, slot) in enumerate(zip(news_in, slots))]
     stores = [pltpu.make_async_copy(slot, dst, store_sem.at[i]) for i, (slot, dst) in enumerate(zip(slots, news_out))]
@@ -707,15 +713,15 @@
             stage_rows(late.at[n], w_up, w_down, obuf.at[place(k)])
             store_micro(k).start()
 
-            @pl.when(n == 0)
+            @pl.when(n == 1)
             def _():
                 for load, store in zip(loads, stores):
                     load.wait()
                     store.start()
             for j in range(per_late):
-                k = per_late * n + j
-
-                @pl.when(k < n_micro - N_LATE)
+                k = per_late * (n - 2) + j
+
+                @pl.when((k >= 0) & (k < n_micro - N_LATE))
                 def _():
                     turn_micro(k, 0)
             return 0

time: 118 us -> 117 us (level)
    pallas_call x1, Pallas kernels: 14.2 us -> 11.5 us  [finish_step(): pl.pallas_call(finish_kernel, name='finish_step', out_shape=[jax.ShapeDty...]
    pallas_call x1, Pallas kernels: 101 us -> 102 us  [fused_step(): pl.pallas_call(step_kernel, name='pipeline_step', out_shape=[jax.ShapeDty...]
where the time goes in v6:
time: 117 us; the launch traced here: 116 us
  Pallas kernels  114 us (97%)
  between operations  2.1 us (2%)
    pallas_call x1, Pallas kernels, fused_step(): pl.pallas_call(step_kernel, name='pipeline_step', out_shape=[jax.ShapeDty...  102 us
    pallas_call x1, Pallas kernels, finish_step(): pl.pallas_call(finish_kernel, name='finish_step', out_shape=[jax.ShapeDty...  11.5 us

profile of v6, /device:TPU:3, one launch (start us, length us, event | category | flops | bytes accessed | tf_op | source)
XLA Modules:
  0.0 115.9 jit_solution(11452094007853919288)
XLA Ops:
  1.9 102.3 %pipeline_step.1 = (bf16[16,1024,256]{2,1,0:T(8,128)(2,1)}, f32[256,1024]{1,0:T(8,128)}, f32[1024,256]{1,0:T(8,128)}, f32[256,1024]{1,0:T(8,128)}, f32[1024,256]...) custom-call(f32[256,1024]{1,0:T(8,128)} %bitcast.20, ...), custom_call_target="tpu_custom_call" | custom-call | tf_op jit(solution)/shard_map/pipeline_step/pallas_call | solution.py:627
  104.2 11.5 %finish_step.1 = (bf16[16,1024,256]{2,1,0:T(8,128)(2,1)}, f32[256,1024]{1,0:T(8,128)}, f32[1024,256]{1,0:T(8,128)}, f32[256,1024]{1,0:T(8,128)}, f32[1024,256]{1...) custom-call(bf16[16,1024,256]{2,1,0:T(8,128)(2,1)} %get-tuple-element.24.outs_in, ...), custom_call_target="tpu_custom_call" | custom-call | tf_op jit(solution)/shard_map/finish_step/pallas_call | solution.py:750

commit v7 on v6

--- a/solution.py
+++ b/solution.py
@@ -17,7 +17,7 @@
 N_SENT = 5
 N_CHUNK = 4
 N_LATE = 6
-N_TWICE = 3
+N_TWICE = 4
 N_PIECE = 1
 MESH = pl.DeviceIdType.MESH
 BF16 = jnp.bfloat16
@@ -448,13 +448,10 @@
         def relays(p):
             return [(up_copy(1 - z, y, 0, p, z_peer), up_copy(1 - z, y, 2, p, y_peer)), (down_copy(z, 1 - y, 3, p, y_peer), down_copy(z, 1 - y, 5, p, z_peer))]
 
-        def begin(fed=None):
+        def begin(matrix):
             for p in range(N_PIECE):
-                for i, sends in enumerate((up_sends(p), down_sends(p))):
-                    if fed is not None:
-                        fed(p)[i].wait_recv()
-                    for c in sends:
-                        c.start()
+                for c in (up_sends, down_sends)[matrix](p):
+                    c.start()
 
         def relay():
             for p in range(N_PIECE):
@@ -492,7 +489,8 @@
 
     @pl.when(stage >= 2)
     def _():
-        mean_begin()
+        mean_begin(0)
+        mean_begin(1)
         mean_relay()
         mean_finish()
 
@@ -508,35 +506,32 @@
     clip = jnp.minimum(1.0, norm_ref[0] / (jnp.sqrt(total) + NORM_EPS))
 
     rate = rate_ref[0]
-    whole = jnp.where(stage >= 2, 1, 0)
 
     def renew(rows, master, moments, mean, weights, scale, first, full):
         new = adamw_update(master[rows, :], moments[0, rows, :], moments[1, rows, :], mean[rows, :], clip, rate)
         if first:
             weights[rows, :] = new[0].astype(BF16) * jnp.asarray(scale, BF16)
 
-        @pl.when(full)
-        def _():
+        if full:
             master[rows, :] = new[0]
             moments[0, rows, :] = new[1]
             moments[1, rows, :] = new[2]
 
-    def renew_block(up_block, down_block, first, full):
-        renew(pl.ds(pl.multiple_of(64 * up_block, 64), 64), up32, m_up, mean_up, up_own, 0.5, first, full)
-        renew(pl.ds(pl.multiple_of(256 * down_block, 256), 256), down32, m_down, mean_down, down_own, 1.0, first, full)
-
-    def renew_first(t, _):
-        renew_block(whole * t + (1 - whole) * (2 * y + z), whole * t + (1 - whole) * (2 * z + y), True, whole == 1)
-        return 0
-
-    def renew_rest(t, _):
-        renew_block(t, t, False, t >= 0)
-        return 0
+    def renew_up(block, first, full):
+        renew(pl.ds(pl.multiple_of(64 * block, 64), 64), up32, m_up, mean_up, up_own, 0.5, first, full)
+
+    def renew_down(block, first, full):
+        renew(pl.ds(pl.multiple_of(256 * block, 256), 256), down32, m_down, mean_down, down_own, 1.0, first, full)
+
+    def renew_all(first):
+        def body(t, _):
+            renew_up(t, first, True)
+            renew_down(t, first, True)
+            return 0
+        lax.fori_loop(0, 4, body, 0)
 
     new_stores = [pltpu.make_async_copy(src, dst, in_sem.at[i]) for i, (src, dst) in enumerate((
         (up32, new_up_hbm), (down32, new_down_hbm), (m_up.at[0], new_m1_up_hbm), (m_down.at[0], new_m1_down_hbm), (m_up.at[1], new_m2_up_hbm), (m_down.at[1], new_m2_down_hbm)))]
-    lax.fori_loop(0, 1 + 3 * whole, renew_first, 0)
-
     def feed(p):
         parts = [(up_own, up_aux, up_rows(z, y, up_piece * p, up_piece)), (down_own, down_aux, down_rows(z, y, down_piece * p, down_piece))]
         return [pltpu.make_async_remote_copy(src_ref=own.at[rows], dst_ref=aux.at[rows], send_sem=aux_send.at[2 * p + i], recv_sem=aux_recv.at[2 * p + i], device_id={"stage": 3 - stage}, device_id_type=MESH)
@@ -544,18 +539,27 @@
 
     @pl.when(stage < 2)
     def _():
+        renew_up(2 * y + z, True, False)
         for p in range(N_PIECE):
-            for c in feed(p):
-                c.start()
-        own_begin()
+            feed(p)[0].start()
+        own_begin(0)
+        renew_down(2 * z + y, True, False)
+        for p in range(N_PIECE):
+            feed(p)[1].start()
+        own_begin(1)
         own_relay()
-        mean_begin()
+        mean_begin(0)
+        mean_begin(1)
 
     @pl.when(stage >= 2)
     def _():
+        for matrix in range(2):
+            for p in range(N_PIECE):
+                feed(p)[matrix].wait_recv()
+            aux_begin(matrix)
+        renew_all(True)
         for copy in new_stores:
             copy.start()
-        aux_begin(feed)
         aux_relay()
 
     def relay_mean(now):
@@ -568,7 +572,7 @@
     @pl.when(stage < 2)
     def _():
         mean_finish()
-        lax.fori_loop(0, 4, renew_rest, 0)
+        renew_all(False)
         for copy in new_stores:
             copy.start()
     store_w_up = pltpu.make_async_copy(up_own, w_up_hbm, in_sem.at[6])

time: 117 us -> 115 us (0.983)
  Pallas kernels: 114 us -> 112 us
    pallas_call x1, Pallas kernels: 102 us -> 101 us  [fused_step(): pl.pallas_call(step_kernel, name='pipeline_step', out_shape=[jax.ShapeDty...]
where the time goes in v7:
time: 115 us; the launch traced here: 114 us
  Pallas kernels  112 us (97%)
  between operations  2.1 us (2%)
    pallas_call x1, Pallas kernels, fused_step(): pl.pallas_call(step_kernel, name='pipeline_step', out_shape=[jax.ShapeDty...  101 us
    pallas_call x1, Pallas kernels, finish_step(): pl.pallas_call(finish_kernel, name='finish_step', out_shape=[jax.ShapeDty...  11.5 us

profile of v7, /device:TPU:3, one launch (start us, length us, event | category | flops | bytes accessed | tf_op | source)
XLA Modules:
  0.0 114.5 jit_solution(5317527788950807144)
XLA Ops:
  1.9 100.9 %pipeline_step.1 = (bf16[16,1024,256]{2,1,0:T(8,128)(2,1)}, f32[256,1024]{1,0:T(8,128)}, f32[1024,256]{1,0:T(8,128)}, f32[256,1024]{1,0:T(8,128)}, f32[1024,256]...) custom-call(f32[256,1024]{1,0:T(8,128)} %bitcast.20, ...), custom_call_target="tpu_custom_call" | custom-call | tf_op jit(solution)/shard_map/pipeline_step/pallas_call | solution.py:631
  102.8 11.5 %finish_step.1 = (bf16[16,1024,256]{2,1,0:T(8,128)(2,1)}, f32[256,1024]{1,0:T(8,128)}, f32[1024,256]{1,0:T(8,128)}, f32[256,1024]{1,0:T(8,128)}, f32[1024,256]{1...) custom-call(bf16[16,1024,256]{2,1,0:T(8,128)(2,1)} %get-tuple-element.24.outs_in, ...), custom_call_target="tpu_custom_call" | custom-call | tf_op jit(solution)/shard_map/finish_step/pallas_call | solution.py:754

commit v8 on v7

--- a/solution.py
+++ b/solution.py
@@ -17,7 +17,7 @@
 N_SENT = 5
 N_CHUNK = 4
 N_LATE = 6
-N_TWICE = 4
+N_TWICE = 5
 N_PIECE = 1
 MESH = pl.DeviceIdType.MESH
 BF16 = jnp.bfloat16
@@ -448,10 +448,10 @@
         def relays(p):
             return [(up_copy(1 - z, y, 0, p, z_peer), up_copy(1 - z, y, 2, p, y_peer)), (down_copy(z, 1 - y, 3, p, y_peer), down_copy(z, 1 - y, 5, p, z_peer))]
 
-        def begin(matrix):
+        def begin(matrix, hops=(0, 1)):
             for p in range(N_PIECE):
-                for c in (up_sends, down_sends)[matrix](p):
-                    c.start()
+                for hop in hops:
+                    (up_sends, down_sends)[matrix](p)[hop].start()
 
         def relay():
             for p in range(N_PIECE):
@@ -542,11 +542,13 @@
         renew_up(2 * y + z, True, False)
         for p in range(N_PIECE):
             feed(p)[0].start()
-        own_begin(0)
+        own_begin(0, (0,))
         renew_down(2 * z + y, True, False)
         for p in range(N_PIECE):
             feed(p)[1].start()
-        own_begin(1)
+        own_begin(1, (0,))
+        own_begin(0, (1,))
+        own_begin(1, (1,))
         own_relay()
         mean_begin(0)
         mean_begin(1)

time: 115 us -> 113 us (0.983)
    pallas_call x1, Pallas kernels: 101 us -> 99.5 us  [fused_step(): pl.pallas_call(step_kernel, name='pipeline_step', out_shape=[jax.ShapeDty...]
where the time goes in v8:
time: 113 us
  Pallas kernels  111 us (98%)
  between operations  2.1 us (2%)
    pallas_call x1, Pallas kernels, fused_step(): pl.pallas_call(step_kernel, name='pipeline_step', out_shape=[jax.ShapeDty...  99.5 us
    pallas_call x1, Pallas kernels, finish_step(): pl.pallas_call(finish_kernel, name='finish_step', out_shape=[jax.ShapeDty...  11.5 us

profile of v8, /device:TPU:3, one launch (start us, length us, event | category | flops | bytes accessed | tf_op | source)
XLA Modules:
  0.0 113.1 jit_solution(15118342279812884169)
XLA Ops:
  1.9 99.5 %pipeline_step.1 = (bf16[16,1024,256]{2,1,0:T(8,128)(2,1)}, f32[256,1024]{1,0:T(8,128)}, f32[1024,256]{1,0:T(8,128)}, f32[256,1024]{1,0:T(8,128)}, f32[1024,256]...) custom-call(f32[256,1024]{1,0:T(8,128)} %bitcast.20, ...), custom_call_target="tpu_custom_call" | custom-call | tf_op jit(solution)/shard_map/pipeline_step/pallas_call | solution.py:633
  101.4 11.5 %finish_step.1 = (bf16[16,1024,256]{2,1,0:T(8,128)(2,1)}, f32[256,1024]{1,0:T(8,128)}, f32[1024,256]{1,0:T(8,128)}, f32[256,1024]{1,0:T(8,128)}, f32[1024,256]{1...) custom-call(bf16[16,1024,256]{2,1,0:T(8,128)(2,1)} %get-tuple-element.24.outs_in, ...), custom_call_target="tpu_custom_call" | custom-call | tf_op jit(solution)/shard_map/finish_step/pallas_call | solution.py:756

commit v9 on v8

--- a/solution.py
+++ b/solution.py
@@ -17,11 +17,18 @@
 N_SENT = 5
 N_CHUNK = 4
 N_LATE = 6
-N_TWICE = 5
-N_PIECE = 1
+N_TWICE = 6
+N_PIECE = 2
 MESH = pl.DeviceIdType.MESH
 BF16 = jnp.bfloat16
 F32 = jnp.float32
+
+
+def repeat(first, end, body):
+    def step(i, _):
+        body(i)
+        return 0
+    lax.fori_loop(first, end, step, 0)
 
 
 def mat_tn(left, right):
@@ -81,34 +88,31 @@
         return lax.rem(j + n_kept, n_micro)
 
     def finish_stores():
-        def body(i, _):
+        def body(i):
             store(i).wait()
-            return 0
-        lax.fori_loop(0, n_micro, body, 0)
+        repeat(0, n_micro, body)
 
     def hand_over():
         return [pltpu.make_async_remote_copy(src_ref=aux, dst_ref=two, send_sem=two_send.at[i], recv_sem=two_recv.at[i], device_id={"stage": 3}, device_id_type=MESH)
                 for i, (aux, two) in enumerate([(up_aux, up_two), (down_aux, down_two)])]
 
     def finish_sends(first, count):
-        def body(i, _):
+        def body(i):
             push(yout, first + i, stage).wait_send()
-            return 0
-        lax.fori_loop(0, count, body, 0)
+        repeat(0, count, body)
 
     @pl.when(stage == 0)
     def _():
         own_ready()
 
-        def body(j, _):
+        def body(j):
             i = rotated(j)
             load(i).wait()
             stage_rows(nbuf.at[i], up_own, down_own, yout.at[i])
             push(yout, i, 1).start()
             store(i).start()
             relay_mean(j == 7)
-            return 0
-        lax.fori_loop(0, n_micro, body, 0)
+        repeat(0, n_micro, body)
         finish_sends(0, n_micro)
         finish_stores()
 
@@ -116,7 +120,7 @@
     def _():
         own_ready()
 
-        def body(j, _):
+        def body(j):
             i = rotated(j)
             arrived(i)
             stage_rows(xin.at[i], up_own, down_own, yout.at[i])
@@ -126,8 +130,7 @@
                 push(yout, i, 2).start()
             store(i).start()
             relay_mean(j == 7)
-            return 0
-        lax.fori_loop(0, n_micro, body, 0)
+        repeat(0, n_micro, body)
         finish_stores()
 
     @pl.when(stage == 2)
@@ -136,7 +139,7 @@
         for copy in hand_over():
             copy.start()
 
-        def body(k, _):
+        def body(k):
             _, i = mixed(k, n_micro)
             arrived(i)
 
@@ -146,8 +149,7 @@
             stage_rows(xin.at[i], up_own, down_own, yout.at[i])
             push(yout, i, 3).start()
             store(i).start()
-            return 0
-        lax.fori_loop(0, n_micro, body, 0)
+        repeat(0, n_micro, body)
         finish_sends(0, n_micro)
         finish_stores()
         for copy in hand_over():
@@ -157,7 +159,7 @@
     def _():
         aux_ready()
 
-        def first(j, _):
+        def first(j):
             load(j).wait()
             stage_rows(nbuf.at[j], up_aux, down_aux, nbuf.at[j])
 
@@ -170,38 +172,33 @@
             def _():
                 stage_rows(nbuf.at[j], up_two, down_two, nbuf.at[j])
             push(nbuf, j, 2).start()
-            return 0
-        lax.fori_loop(0, n_kept, first, 0)
-
-        def body(k, _):
+        repeat(0, n_kept, first)
+
+        def body(k):
             _, i = mixed(k, n_micro)
             arrived(i)
             stage_rows(xin.at[i], up_own, down_own, yout.at[i])
             store(i).start()
-            return 0
-        lax.fori_loop(0, n_micro - N_LATE, body, 0)
+        repeat(0, n_micro - N_LATE, body)
 
         def late(k):
             _, i = mixed(k, n_micro)
             return i, pltpu.make_async_copy(xin.at[i], late_hbm.at[k - (n_micro - N_LATE)], out_sem.at[i])
 
-        def save(k, _):
+        def save(k):
             i, copy = late(k)
             arrived(i)
             copy.start()
-            return 0
-        lax.fori_loop(n_micro - N_LATE, n_micro, save, 0)
-
-        def stored(k, _):
+        repeat(n_micro - N_LATE, n_micro, save)
+
+        def stored(k):
             _, i = mixed(k, n_micro)
             store(i).wait()
-            return 0
-        lax.fori_loop(0, n_micro - N_LATE, stored, 0)
-
-        def saved(k, _):
+        repeat(0, n_micro - N_LATE, stored)
+
+        def saved(k):
             late(k)[1].wait()
-            return 0
-        lax.fori_loop(n_micro - N_LATE, n_micro, saved, 0)
+        repeat(n_micro - N_LATE, n_micro, saved)
         finish_sends(0, n_kept)
 
 
@@ -209,18 +206,17 @@
     n_micro = nbuf.shape[0]
     n_kept = n_micro - N_SENT
 
-    def body(j, _):
+    def body(j):
         i = lax.rem(j + n_kept, n_micro)
         pltpu.make_async_copy(nb_hbm.at[i], nbuf.at[i], nb_sem.at[i]).start()
-        return 0
 
     @pl.when(stage == 0)
     def _():
-        lax.fori_loop(0, n_micro, body, 0)
+        repeat(0, n_micro, body)
 
     @pl.when(stage == 3)
     def _():
-        lax.fori_loop(N_SENT, n_micro, body, 0)
+        repeat(N_SENT, n_micro, body)
 
 
 def step_kernel(up_hbm, down_hbm, m1_up_hbm, m1_down_hbm, m2_up_hbm, m2_down_hbm, gu_hbm, gv_hbm, acts_hbm, loss_hbm, nb_hbm, rate_ref, norm_ref,
@@ -246,17 +242,9 @@
         return pl.ds(pl.multiple_of(512 * zz + 256 * yy + first, 128), count)
 
     own_up, own_down = up_rows(z, y), down_rows(z, y)
-    loads = [
-        pltpu.make_async_copy(acts_hbm, acts, in_sem.at[0]),
-        pltpu.make_async_copy(up_hbm, up32, in_sem.at[1]),
-        pltpu.make_async_copy(down_hbm, down32, in_sem.at[2]),
-        pltpu.make_async_copy(gv_hbm, gv, in_sem.at[3]),
-        pltpu.make_async_copy(gu_hbm, gu, in_sem.at[4]),
-        pltpu.make_async_copy(m1_up_hbm, m_up.at[0], in_sem.at[5]),
-        pltpu.make_async_copy(m2_up_hbm, m_up.at[1], in_sem.at[6]),
-        pltpu.make_async_copy(m1_down_hbm, m_down.at[0], in_sem.at[7]),
-        pltpu.make_async_copy(m2_down_hbm, m_down.at[1], in_sem.at[8]),
-    ]
+    loads = [pltpu.make_async_copy(src, dst, in_sem.at[i]) for i, (src, dst) in enumerate((
+        (acts_hbm, acts), (up_hbm, up32), (down_hbm, down32), (gv_hbm, gv), (gu_hbm, gu),
+        (m1_up_hbm, m_up.at[0]), (m2_up_hbm, m_up.at[1]), (m1_down_hbm, m_down.at[0]), (m2_down_hbm, m_down.at[1])))]
     load_loss = pltpu.make_async_copy(loss_hbm, gbuf, in_sem.at[9])
     for copy in loads[:2]:
         copy.start()
@@ -268,11 +256,10 @@
 
     barrier = pltpu.get_barrier_semaphore()
 
-    def greet(d, _):
+    def greet(d):
         other = lax.rem(me + d, 16)
         pl.semaphore_signal(barrier, inc=1, device_id={"data": lax.div(other, 4), "stage": lax.rem(other, 4)}, device_id_type=MESH)
-        return 0
-    lax.fori_loop(1, 16, greet, 0)
+    repeat(1, 16, greet)
 
     def chunk_rows(k):
         return pl.ds(pl.multiple_of(k * chunk, chunk), chunk)
@@ -332,7 +319,7 @@
             loads[3].wait()
             loads[4].wait()
 
-        def half(h, _):
+        def half(h):
             zz = h * z + (1 - h) * (1 - z)
             yy = h * y + (1 - h) * (1 - y)
             send = (k == N_CHUNK - 1) & (h == 0)
@@ -352,10 +339,9 @@
                 for sub in range(2):
                     for c in range(2):
                         u_first(sub, c).start()
-            return 0
-        lax.fori_loop(0, 2, half, 0)
-
-    def tick(t, _):
+        repeat(0, 2, half)
+
+    def tick(t):
         upper = jnp.where(stage >= 2, 1, 0)
         even = 1 - lax.rem(t, 2)
         early = jnp.where(t < N_CHUNK, 1, 0)
@@ -375,7 +361,6 @@
         @pl.when(is_grad == 1)
         def _():
             add_grads(k)
-        return 0
 
     loads[0].wait()
     loads[1].wait()
@@ -391,7 +376,7 @@
     @pl.when(stage == 3)
     def _():
         load_loss.wait()
-    lax.fori_loop(1, 3 * N_CHUNK, tick, 0)
+    repeat(1, 3 * N_CHUNK, tick)
 
     for c in range(2):
         v_first(0, c).wait_recv()
@@ -480,10 +465,9 @@
 
     sq_all[me] = acc
 
-    def tell(d, _):
+    def tell(d):
         sq_copy(lax.rem(me + d, 16), me).start()
-        return 0
-    lax.fori_loop(1, 16, tell, 0)
+    repeat(1, 16, tell)
     for copy in loads[5:]:
         copy.wait()
 
@@ -494,11 +478,10 @@
         mean_relay()
         mean_finish()
 
-    def hear(d, _):
+    def hear(d):
         other = lax.rem(me + d, 16)
         sq_copy(other, other).wait_recv()
-        return 0
-    lax.fori_loop(1, 16, hear, 0)
+    repeat(1, 16, hear)
     total = sq_all[0]
     for i in range(1, 16):
         total = total + sq_all[i]
@@ -524,11 +507,10 @@
         renew(pl.ds(pl.multiple_of(256 * block, 256), 256), down32, m_down, mean_down, down_own, 1.0, first, full)
 
     def renew_all(first):
-        def body(t, _):
+        def body(t):
             renew_up(t, first, True)
             renew_down(t, first, True)
-            return 0
-        lax.fori_loop(0, 4, body, 0)
+        repeat(0, 4, body)
 
     new_stores = [pltpu.make_async_copy(src, dst, in_sem.at[i]) for i, (src, dst) in enumerate((
         (up32, new_up_hbm), (down32, new_down_hbm), (m_up.at[0], new_m1_up_hbm), (m_down.at[0], new_m1_down_hbm), (m_up.at[1], new_m2_up_hbm), (m_down.at[1], new_m2_down_hbm)))]
@@ -584,10 +566,9 @@
 
     @pl.when(stage == 1)
     def _():
-        def left(i, _):
+        def left(i):
             pltpu.make_async_remote_copy(src_ref=yout.at[i], dst_ref=xin.at[i], send_sem=send_sem.at[i], recv_sem=recv_sem.at[i], device_id={"stage": 2}, device_id_type=MESH).wait_send()
-            return 0
-        lax.fori_loop(nbuf.shape[0] - N_SENT, nbuf.shape[0], left, 0)
+        repeat(nbuf.shape[0] - N_SENT, nbuf.shape[0], left)
 
     @pl.when(stage > 0)
     def _():
@@ -600,10 +581,9 @@
         v_second(c).wait_send()
         u_second(c).wait_send()
 
-    def told(d, _):
+    def told(d):
         sq_copy(lax.rem(me + d, 16), me).wait_send()
-        return 0
-    lax.fori_loop(1, 16, told, 0)
+    repeat(1, 16, told)
     mean_drain()
 
     @pl.when(stage < 2)
@@ -652,8 +632,7 @@
             vmem((width, hidden), BF16), vmem((hidden, width), BF16),
             vmem((16, 8, 128), F32),
             vmem(next_batch.shape, BF16), vmem(next_batch.shape, BF16), vmem(next_batch.shape, BF16),
-            dma((10,)), dma((N_CHUNK,)), dma((N_CHUNK,)), dma((12,)), dma((12,)), dma((16,)), dma((16,)), dma((18 * N_PIECE,)), dma((18 * N_PIECE,)), dma((2 * N_PIECE,)), dma((2 * N_PIECE,)),
-            dma((n_micro,)), dma((n_micro,)), dma((n_micro,)), dma((n_micro,)), dma((2,)), dma((2,)),
+            *(dma((n,)) for n in (10, N_CHUNK, N_CHUNK, 12, 12, 16, 16, 18 * N_PIECE, 18 * N_PIECE, 2 * N_PIECE, 2 * N_PIECE, n_micro, n_micro, n_micro, n_micro, 2, 2)),
         ],
         compiler_params=pltpu.CompilerParams(collective_id=1, has_side_effects=True, vmem_limit_bytes=63 * 1024 * 1024),
     )(master_up, master_down, m1_up, m1_down, m2_up, m2_down, grad_up, grad_down, acts, loss_grad, next_batch, learn_rate, max_norm)
@@ -686,34 +665,31 @@
     def load_late(n):
         return pltpu.make_async_copy(late_in.at[n], late.at[n], late_load.at[n])
 
-    def start_micro(k, _):
+    def start_micro(k):
         load_micro(k).start()
-        return 0
-
-    def turn_micro(k, _):
+
+    def turn_micro(k):
         load_micro(k).wait()
         store_micro(k).start()
-        return 0
-
-    def start_late(n, _):
+
+    def start_late(n):
         load_late(n).start()
-        return 0
 
     @pl.when(last)
     def _():
         for copy in w_loads:
             copy.start()
-        lax.fori_loop(0, N_LATE, start_late, 0)
+        repeat(0, N_LATE, start_late)
     for copy in loads:
         copy.start()
-    lax.fori_loop(0, n_copied, start_micro, 0)
+    repeat(0, n_copied, start_micro)
 
     @pl.when(last)
     def _():
         for copy in w_loads:
             copy.wait()
 
-        def body(n, _):
+        def body(n):
             load_late(n).wait()
             k = n_micro - N_LATE + n
             stage_rows(late.at[n], w_up, w_down, obuf.at[place(k)])
@@ -729,21 +705,19 @@
 
                 @pl.when((k >= 0) & (k < n_micro - N_LATE))
                 def _():
-                    turn_micro(k, 0)
-            return 0
-        lax.fori_loop(0, N_LATE, body, 0)
+                    turn_micro(k)
+        repeat(0, N_LATE, body)
 
     @pl.when(jnp.logical_not(last))
     def _():
         for load, store in zip(loads, stores):
             load.wait()
             store.start()
-        lax.fori_loop(0, n_micro, turn_micro, 0)
-
-    def stored(k, _):
+        repeat(0, n_micro, turn_micro)
+
+    def stored(k):
         store_micro(k).wait()
-        return 0
-    lax.fori_loop(0, n_micro, stored, 0)
+    repeat(0, n_micro, stored)
     for copy in stores:
         copy.wait()
 

time: 113 us -> 112 us (level)
  no operation moved by 1% of the time
where the time goes in v9:
time: 112 us
  Pallas kernels  110 us (98%)
  between operations  2.1 us (2%)
    pallas_call x1, Pallas kernels, fused_step(): pl.pallas_call(step_kernel, name='pipeline_step', out_shape=[jax.ShapeDty...  98.4 us
    pallas_call x1, Pallas kernels, finish_step(): pl.pallas_call(finish_kernel, name='finish_step', out_shape=[jax.ShapeDty...  11.5 us

profile of v9, /device:TPU:3, one launch (start us, length us, event | category | flops | bytes accessed | tf_op | source)
XLA Modules:
  0.0 112.0 jit_solution(17305169854348505446)
XLA Ops:
  1.9 98.4 %pipeline_step.1 = (bf16[16,1024,256]{2,1,0:T(8,128)(2,1)}, f32[256,1024]{1,0:T(8,128)}, f32[1024,256]{1,0:T(8,128)}, f32[256,1024]{1,0:T(8,128)}, f32[1024,256]...) custom-call(f32[256,1024]{1,0:T(8,128)} %bitcast.20, ...), custom_call_target="tpu_custom_call" | custom-call | tf_op jit(solution)/shard_map/pipeline_step/pallas_call | solution.py:613
  100.3 11.5 %finish_step.1 = (bf16[16,1024,256]{2,1,0:T(8,128)(2,1)}, f32[256,1024]{1,0:T(8,128)}, f32[1024,256]{1,0:T(8,128)}, f32[256,1024]{1,0:T(8,128)}, f32[1024,256]{1...) custom-call(bf16[16,1024,256]{2,1,0:T(8,128)(2,1)} %get-tuple-element.24.outs_in, ...), custom_call_target="tpu_custom_call" | custom-call | tf_op jit(solution)/shard_map/finish_step/pallas_call | solution.py:730

commit v10 on v9

--- a/solution.py
+++ b/solution.py
@@ -17,7 +17,7 @@
 N_SENT = 5
 N_CHUNK = 4
 N_LATE = 6
-N_TWICE = 6
+N_TWICE = 5
 N_PIECE = 2
 MESH = pl.DeviceIdType.MESH
 BF16 = jnp.bfloat16

time: 112 us -> 111 us (level)
  Pallas kernels: 110 us -> 108 us
    pallas_call x1, Pallas kernels: 98.4 us -> 97 us  [fused_step(): pl.pallas_call(step_kernel, name='pipeline_step', out_shape=[jax.ShapeDty...]
where the time goes in v10:
time: 111 us
  Pallas kernels  108 us (97%)
  between operations  2.1 us (2%)
    pallas_call x1, Pallas kernels, fused_step(): pl.pallas_call(step_kernel, name='pipeline_step', out_shape=[jax.ShapeDty...  97 us
    pallas_call x1, Pallas kernels, finish_step(): pl.pallas_call(finish_kernel, name='finish_step', out_shape=[jax.ShapeDty...  11.5 us

profile of v10, /device:TPU:3, one launch (start us, length us, event | category | flops | bytes accessed | tf_op | source)
XLA Modules:
  0.0 110.6 jit_solution(14633998720193875020)
XLA Ops:
  1.9 97.0 %pipeline_step.1 = (bf16[16,1024,256]{2,1,0:T(8,128)(2,1)}, f32[256,1024]{1,0:T(8,128)}, f32[1024,256]{1,0:T(8,128)}, f32[256,1024]{1,0:T(8,128)}, f32[1024,256]...) custom-call(f32[256,1024]{1,0:T(8,128)} %bitcast.20, ...), custom_call_target="tpu_custom_call" | custom-call | tf_op jit(solution)/shard_map/pipeline_step/pallas_call | solution.py:613
  98.9 11.5 %finish_step.1 = (bf16[16,1024,256]{2,1,0:T(8,128)(2,1)}, f32[256,1024]{1,0:T(8,128)}, f32[1024,256]{1,0:T(8,128)}, f32[256,1024]{1,0:T(8,128)}, f32[1024,256]{1...) custom-call(bf16[16,1024,256]{2,1,0:T(8,128)(2,1)} %get-tuple-element.24.outs_in, ...), custom_call_target="tpu_custom_call" | custom-call | tf_op jit(solution)/shard_map/finish_step/pallas_call | solution.py:730
